TPU v7x, 256 devices: a whole 4x4x8 slice. The times are simulated.
256 devices in a mesh: dp: 8 (over x, y_lo), fsdp: 32 (over z, y_hi, core).
Axes of the slice: x: 4, y: 4 (y_hi: 2, y_lo: 2; y = y_hi * 2 + y_lo), z: 8, core: 2. Of those that a mesh axis runs over, the one named last changes fastest.
Arguments:
- hidden: bfloat16 [131072, 4096], P(('dp', 'fsdp')), may hold values from -24 to 24
- queries: bfloat16 [131072, 2048], P(('dp', 'fsdp')), may hold values from -60 to 60
- cotangent: bfloat16 [131072, 2048], P(('dp', 'fsdp')), may hold values from -0.0390625 to 0.0390625
- point_start: bfloat16 [4096, 1024], P('fsdp', 'dp'), may hold values from -0.09375 to 0.09375
- point_mid: bfloat16 [4096, 1024], P('fsdp', 'dp'), may hold values from -0.09375 to 0.09375
- point_end: bfloat16 [4096, 1024], P('fsdp', 'dp'), may hold values from -0.09375 to 0.09375
- curve_time: float32 [1], replicated, may hold values from 0.15 to 0.85
Outputs:
- context: bfloat16 [131072, 2048], P(('dp', 'fsdp'))
- gradient: float32 [4096, 1024], P('fsdp', 'dp')
All inputs are finite; a program needn't handle non-finite values.
Results may differ from a plain program's by a relative error of at most 0.0071.
Values may be sent and summed in bfloat16 or wider, within the bound.
A program may use at most 128 MiB of HBM per device.

v0:
```python
import math

import jax
import jax.numpy as jnp
from jax import lax
from jax.sharding import PartitionSpec as P

KVH = 4
HD = 128


def laid_out(tiles, dim):
    tiles = jnp.moveaxis(tiles, 0, dim)
    shape = tiles.shape
    return tiles.reshape(*shape[:dim], shape[dim] * shape[dim + 1], *shape[dim + 2 :])


def copy_for_each(array, axis):
    devices = lax.axis_size(axis)
    return lax.all_to_all(
        jnp.broadcast_to(array[None], (devices, *array.shape)), axis, 0, 0, tiled=True
    )


def gathered_copies(array, axis, dim):
    return laid_out(copy_for_each(array, axis), dim)


def in_blocks(array, dim, devices):
    shape = array.shape
    tiles = array.reshape(*shape[:dim], devices, shape[dim] // devices, *shape[dim + 1 :])
    return jnp.moveaxis(tiles, dim, 0)


def summed_on_arrival(array, axis, dim):
    devices = lax.axis_size(axis)
    tiles = lax.all_to_all(in_blocks(array, dim, devices), axis, 0, 0, tiled=True)
    return jnp.sum(tiles, axis=0)


def rope_tables(seq_len, head_dim):
    positions = jnp.arange(seq_len, dtype=jnp.float32)[:, None]
    halves_index = jnp.arange(head_dim // 2, dtype=jnp.float32)[None, :]
    inverse = jnp.exp(-(2.0 * halves_index / head_dim) * math.log(500000.0))
    angles = positions * inverse
    cosine = jnp.concatenate([jnp.cos(angles), jnp.cos(angles)], axis=1)
    sine_t = jnp.concatenate([jnp.sin(angles), jnp.sin(angles)], axis=1)
    return (cosine, sine_t)


def rotate(values_in):
    half_size = values_in.shape[-1] // 2
    return jnp.concatenate([-values_in[..., half_size:], values_in[..., :half_size]], axis=-1)


def rotate_back(values_in):
    half_size = values_in.shape[-1] // 2
    return jnp.concatenate([values_in[..., half_size:], -values_in[..., :half_size]], axis=-1)


def attend(kv_rows, query_rows, grad_rows, kv_heads, head_dim):
    seq_len = kv_rows.shape[0]
    kv_width = kv_heads * head_dim
    group_size = query_rows.shape[1] // kv_width
    width_head = group_size * head_dim
    cosine, sine_t = rope_tables(seq_len, head_dim)
    causal = jnp.arange(seq_len)[:, None] >= jnp.arange(seq_len)[None, :]
    score_scale = 1.0 / math.sqrt(head_dim)
    contexts = []
    key_grads = []
    value_grads = []
    for kv_head in range(kv_heads):
        keys_raw = kv_rows[:, kv_head * head_dim : (kv_head + 1) * head_dim].astype(jnp.float32)
        values_head = kv_rows[
            :, kv_width + kv_head * head_dim : kv_width + (kv_head + 1) * head_dim
        ]
        keys_head = (keys_raw * cosine + rotate(keys_raw) * sine_t).astype(jnp.bfloat16)
        query_head = query_rows[:, kv_head * width_head : (kv_head + 1) * width_head].reshape(
            seq_len, group_size, head_dim
        )
        grad_head = grad_rows[:, kv_head * width_head : (kv_head + 1) * width_head].reshape(
            seq_len, group_size, head_dim
        )
        scores = (
            jnp.einsum("sgd,td->gst", query_head, keys_head, preferred_element_type=jnp.float32)
            * score_scale
        )
        scores = jnp.where(causal[None], scores, -1e30)
        top_score = jnp.max(scores, axis=-1, keepdims=True)
        weights_exp = jnp.exp(scores - top_score)
        probs = weights_exp / jnp.sum(weights_exp, axis=-1, keepdims=True)
        probs_low = probs.astype(jnp.bfloat16)
        context_head = jnp.einsum(
            "gst,td->sgd", probs_low, values_head, preferred_element_type=jnp.float32
        ).astype(jnp.bfloat16)
        contexts.append(context_head.reshape(seq_len, width_head))
        prob_grad = jnp.einsum(
            "sgd,td->gst", grad_head, values_head, preferred_element_type=jnp.float32
        )
        value_grads.append(
            jnp.einsum("gst,sgd->td", probs_low, grad_head, preferred_element_type=jnp.float32)
        )
        score_grad = (
            probs * (prob_grad - jnp.sum(prob_grad * probs, axis=-1, keepdims=True)) * score_scale
        )
        score_low = score_grad.astype(jnp.bfloat16)
        rot_grad = jnp.einsum(
            "gst,sgd->td", score_low, query_head, preferred_element_type=jnp.float32
        )
        key_grads.append(rot_grad * cosine + rotate_back(rot_grad * sine_t))
    context_rows = jnp.concatenate(contexts, axis=1)
    kv_grad = jnp.concatenate(key_grads + value_grads, axis=1).astype(jnp.bfloat16)
    return (context_rows, kv_grad)


def local(hidden, queries, cotangent, point_start, point_mid, point_end, curve_time):
    t_value = curve_time[0]
    blended = (
        (1.0 - t_value) ** 2 * point_start.astype(jnp.float32)
        + 2.0 * t_value * (1.0 - t_value) * point_mid.astype(jnp.float32)
        + t_value**2 * point_end.astype(jnp.float32)
    ).astype(jnp.bfloat16)
    columns_full = gathered_copies(blended, "dp", 1)
    window = hidden
    kv_sum = jnp.dot(
        window,
        lax.all_gather(columns_full, "fsdp", axis=0, tiled=True),
        preferred_element_type=jnp.float32,
    )
    kv_rows = kv_sum.astype(jnp.bfloat16)
    context, kv_grad = attend(kv_rows, queries, cotangent, KVH, HD)
    bernstein = 2.0 * t_value * (1.0 - t_value)
    window = hidden
    row_part = lax.psum_scatter(
        jnp.dot(window.T, kv_grad, preferred_element_type=jnp.float32),
        "fsdp",
        scatter_dimension=0,
        tiled=True,
    )
    gradient = summed_on_arrival(row_part, "dp", 1)
    return (context, gradient * bernstein)


def solution(mesh):
    return jax.shard_map(
        local,
        mesh=mesh,
        in_specs=(
            P(("dp", "fsdp"), None),
            P(("dp", "fsdp"), None),
            P(("dp", "fsdp"), None),
            P("fsdp", "dp"),
            P("fsdp", "dp"),
            P("fsdp", "dp"),
            P(),
        ),
        out_specs=(P(("dp", "fsdp"), None), P("fsdp", "dp")),
        check_vma=False,
    )
```

profile of v0, /device:TPU:2, one launch (start us, length us, event | category | flops | bytes accessed | tf_op | source)
XLA Modules:
  0.0 469.1 jit_solution(176603767008599555)
XLA Ops:
  7.9 0.9 copy.70
  8.7 0.9 copy.71
  9.6 0.9 copy.72
  10.6 11.3 %all_to_all.10 = bf16[8,128,128]{1,2,0:T(8,128)(2,1)} all-to-all(bf16[8,128,128]{1,2,0:T(8,128)(2,1)S(1)} %broadcast_in_dim.56), channel_id=1, replica_groups=mesh['dp'=8,'fsdp'=32] {'dp'}, dimensions={0} | all-to-all | bytes 524288 | tf_op jit(solution)/shard_map/all_to_all | solution.py:20
  21.9 2.8 fusion.159
  24.7 2.1 copy.150
  26.8 2.0 copy.152
  28.9 1.0 copy.151
  29.9 1.0 copy.153
  30.9 1.2 fusion.158
  32.1 1.3 copy.157
  33.4 0.2 copy.156
  33.6 0.2 copy.155
  33.8 1.3 copy.154
  35.1 0.8 iota_compare_fusion
  35.9 0.5 fusion.136
  36.4 95.9 %all-gather.2.cloned.1.call-done = bf16[4096,1024]{0,1:T(8,128)(2,1)} async-done(((bf16[128,1024]{0,1:T(8,128)(2,1)}), bf16[4096,1024]{0,1:T(8,128)(2,1)}) %all-gather.2.cloned.1.call-update) | async-done | bytes 8388624 | tf_op jit(solution)/shard_map/all_gather | solution.py:127
  132.3 9.1 %fusion.44 = bf16[512,1024]{0,1:T(8,128)(2,1)S(1)} fusion(bf16[4096,1024]{0,1:T(8,128)(2,1)} %all-gather.2.cloned.1.call-done, bf16[512,4096]{1,0:T(8,128)(2,1)} %param.7), kind=kOutput, calls=%fused_computation.67 | convolution fusion | flops 4295491584 | bytes 13631488 | tf_op jit(solution)/shard_map/dot_general | solution.py:125
  141.4 0.1 slice_convert_fusion.3
  141.5 2.7 fusion.138
  144.2 2.7 fusion.139
  146.9 2.7 fusion.140
  149.6 2.7 fusion.141
  152.3 0.8 slice_negate_fusion.6
  153.1 0.8 fusion.86
  153.9 4.7 %fusion.164 = (f32[4,512]{1,0:T(4,128)S(1)}, f32[4,512,512]{1,2,0:T(8,128)}) fusion(pred[512,512]{0,1:T(8,128)(4,1)} %iota_compare_fusion, bf16[512,4,128]{0,2,1:T(8,128)(2,1)} %bitcast.294, bf16[512,128]{0,1:T(8,128)(2,1)} %get-tuple-element.15), kind=kOutput, calls=%fused_computation.199 | convolution fusion | flops 272630272 | bytes 5120000 | tf_op jit(solution)/shard_map/sub | solution.py:90
  158.7 1.8 fusion.82
  160.5 5.0 %fusion.174 = (f32[4,512]{1,0:T(4,128)S(1)}, f32[4,512,512]{1,2,0:T(8,128)}) fusion(pred[512,512]{0,1:T(8,128)(4,1)} %iota_compare_fusion, bf16[512,4,128]{0,2,1:T(8,128)(2,1)} %bitcast.300, bf16[512,128]{0,1:T(8,128)(2,1)} %get-tuple-element.13), kind=kOutput, calls=%fused_computation.201 | convolution fusion | flops 272630272 | bytes 5120000 | tf_op jit(solution)/shard_map/sub | solution.py:90
  165.5 5.3 %fusion.169 = (f32[4,512]{1,0:T(4,128)}, f32[4,512,512]{1,2,0:T(8,128)}) fusion(pred[512,512]{0,1:T(8,128)(4,1)} %iota_compare_fusion, bf16[512,4,128]{0,2,1:T(8,128)(2,1)} %bitcast.296, bf16[512,128]{0,1:T(8,128)(2,1)S(1)} %copy-done.2), kind=kOutput, calls=%fused_computation.200 | convolution fusion | flops 272630272 | bytes 5120000 | tf_op jit(solution)/shard_map/sub | solution.py:90
  170.8 4.8 %fusion.179 = (f32[4,512]{1,0:T(4,128)S(1)}, f32[4,512,512]{1,2,0:T(8,128)}) fusion(pred[512,512]{0,1:T(8,128)(4,1)} %iota_compare_fusion, bf16[512,4,128]{0,2,1:T(8,128)(2,1)} %bitcast.298, bf16[512,128]{0,1:T(8,128)(2,1)} %get-tuple-element.12), kind=kOutput, calls=%fused_computation.202 | convolution fusion | flops 272630272 | bytes 5120000 | tf_op jit(solution)/shard_map/sub | solution.py:90
  175.6 8.2 %fusion.48 = f32[512,128]{0,1:T(8,128)} fusion(bf16[512,4,128]{0,2,1:T(8,128)(2,1)} %bitcast.299, f32[512,512,4]{1,0,2:T(8,128)} %fusion.138, f32[4,512,512]{1,2,0:T(8,128)} %get-tuple-element.49, f32[4,512]{1,0:T(4,128)S(1)} %get-tuple-element.48), kind=kOutput, calls=%fused_computation.75 | convolution fusion | flops 275778048 | bytes 9183232 | tf_op jit(solution)/shard_map/gst,sgd->td/dot_general | solution.py:107
  183.8 8.4 %fusion.47 = f32[512,128]{0,1:T(8,128)} fusion(bf16[512,4,128]{0,2,1:T(8,128)(2,1)} %bitcast.301, f32[512,512,4]{1,0,2:T(8,128)} %fusion.139, f32[4,512,512]{1,2,0:T(8,128)} %get-tuple-element.47, f32[4,512]{1,0:T(4,128)S(1)} %get-tuple-element.46), kind=kOutput, calls=%fused_computation.74 | convolution fusion | flops 275778048 | bytes 9183232 | tf_op jit(solution)/shard_map/gst,sgd->td/dot_general | solution.py:107
  192.2 8.3 %fusion.46 = f32[512,128]{0,1:T(8,128)} fusion(bf16[512,4,128]{0,2,1:T(8,128)(2,1)} %bitcast.297, f32[512,512,4]{1,0,2:T(8,128)} %fusion.140, f32[4,512,512]{1,2,0:T(8,128)} %get-tuple-element.45, f32[4,512]{1,0:T(4,128)S(1)} %copy-done.10), kind=kOutput, calls=%fused_computation.73 | convolution fusion | flops 275778048 | bytes 9183232 | tf_op jit(solution)/shard_map/gst,sgd->td/dot_general | solution.py:107
  200.5 8.9 %fusion.97 = (f32[512,128]{0,1:T(8,128)}, f32[512,128]{0,1:T(8,128)}, f32[512,128]{0,1:T(8,128)}, f32[512,128]{0,1:T(8,128)}, f32[512,128]{0,1:T(8,128)}) fusion(f32[512,64]{0,1:T(8,128)S(1)} %get-tuple-element.40, f32[512,128]{0,1:T(8,128)} %fusion.48, f32[512,128]{0,1:T(8,128)} %fusion.47, f32[512,128]{0,1:T(8,128)} %fusion.46, ...), kind=kOutput, calls=%fused_computation.128 | convolution fusion | flops 276105728 | bytes 11149312 | tf_op jit(solution)/shard_map/gst,sgd->td/dot_general | solution.py:107
  209.4 1.1 fusion.160
  210.6 1.3 fusion.163
  211.9 1.0 fusion.162
  212.9 1.0 fusion.161
  213.9 1.0 fusion.107
  214.9 1.0 fusion.106
  215.9 1.0 fusion.105
  217.0 0.8 fusion.50
  217.9 1.3 copy-done.6
  219.2 0.8 fusion.52
  220.0 1.3 copy-done.8
  221.4 0.8 fusion.54
  222.2 1.3 copy-done.4
  223.6 0.8 fusion.56
  224.4 1.3 copy-done.3
  225.8 8.1 %convolution_bitcast_fusion = f32[4096,1024]{0,1:T(8,128)} fusion(bf16[512,1024]{0,1:T(8,128)(2,1)S(1)} %fusion.56, bf16[512,4096]{1,0:T(8,128)(2,1)S(1)} %copy-done.3), kind=kOutput, calls=%fused_computation.8 | convolution fusion | flops 4294967296 | bytes 22020096 | tf_op jit(solution)/shard_map/dot_general | solution.py:135
  233.8 2.8 convolution_convert_fusion.1
  236.6 0.6 copy-done.7
  237.3 0.5 convolution_convert_fusion.3
  237.8 1.7 copy-done.9
  239.5 0.5 convolution_convert_fusion.2
  240.0 209.7 %reduce-scatter.2.cloned.1.call-done = f32[128,1024]{0,1:T(8,128)} async-done(((f32[4096,1024]{0,1:T(8,128)}), f32[128,1024]{0,1:T(8,128)}) %reduce-scatter.2.cloned.1.call-update) | async-done | bytes 524304 | tf_op jit(solution)/shard_map/reduce_scatter | solution.py:134
  449.6 4.9 %all-to-all-start.1 = ((f32[8,128,128]{1,2,0:T(8,128)}), f32[8,128,128]{1,2,0:T(8,128)S(1)}, u32[]{:S(2)}, u32[]{:S(2)}) async-start(f32[8,128,128]{1,2,0:T(8,128)} %bitcast.302), calls=%async_computation.2 | async-start | bytes 1048576 | tf_op jit(solution)/shard_map/all_to_all | solution.py:37
  454.5 3.4 convolution_convert_fusion.4
  457.9 0.2 copy.92
  458.1 0.2 copy.90
  458.4 0.2 copy.91
  458.6 1.3 copy.89
  459.8 1.6 pad_maximum_fusion
  461.5 0.7 copy.113
  (28 shorter events, 0.4 us)
Async XLA Ops:
  7.2 125.1 %all-gather.2.cloned.1.call-start = ((), (), s32[]{:S(2)}) async-start(), calls=%async_computation.3 | async-start | bytes 8650752 | tf_op jit(solution)/shard_map/all_gather | solution.py:127
  21.8 9.0 %copy-start = (bf16[512,2048]{1,0:T(8,128)(2,1)S(1)}, bf16[512,2048]{1,0:T(8,128)(2,1)}, u32[]{:S(2)}) copy-start(bf16[512,2048]{1,0:T(8,128)(2,1)} %param.9) | copy-start | bytes 6291460
  21.9 427.8 %reduce-scatter.2.cloned.1.call-start = ((), (), s32[]{:S(2)}) async-start(), calls=%async_computation.4 | async-start | bytes 17301504 | tf_op jit(solution)/shard_map/reduce_scatter | solution.py:134
  160.5 5.0 %copy-start.2 = (bf16[512,128]{0,1:T(8,128)(2,1)S(1)}, bf16[512,128]{0,1:T(8,128)(2,1)}, u32[]{:S(2)}) copy-start(bf16[512,128]{0,1:T(8,128)(2,1)} %get-tuple-element.14) | copy-start | bytes 393220
  183.8 8.4 %copy-start.10 = (f32[4,512]{1,0:T(4,128)S(1)}, f32[4,512]{1,0:T(4,128)}, u32[]{:S(2)}) copy-start(f32[4,512]{1,0:T(4,128)} %get-tuple-element.44) | copy-start | bytes 24580
  209.4 7.5 %copy-start.1 = (f32[512,128]{0,1:T(8,128)S(1)}, f32[512,128]{0,1:T(8,128)}, u32[]{:S(2)}) copy-start(f32[512,128]{0,1:T(8,128)} %get-tuple-element.50) | copy-start | bytes 786436
  209.4 7.6 %copy-start.5 = (f32[4,512,512]{1,2,0:T(8,128)S(1)}, f32[4,512,512]{1,2,0:T(8,128)}, u32[]{:S(2)}) copy-start(f32[4,512,512]{1,2,0:T(8,128)} %get-tuple-element.49) | copy-start | bytes 12582916
  217.0 2.2 copy-start.6
  219.2 2.2 copy-start.8
  221.4 2.2 copy-start.4
  223.6 2.2 copy-start.3
  233.8 3.5 copy-start.7
  237.3 2.2 copy-start.9
  449.6 11.8 %all-to-all-start.1 = ((f32[8,128,128]{1,2,0:T(8,128)}), f32[8,128,128]{1,2,0:T(8,128)S(1)}, u32[]{:S(2)}, u32[]{:S(2)}) async-start(f32[8,128,128]{1,2,0:T(8,128)} %bitcast.302), calls=%async_computation.2 | async-start | bytes 1048576 | tf_op jit(solution)/shard_map/all_to_all | solution.py:37
Sparse Core Ops, SparseCore 0:
  22.0 110.2 all-gather.1
  234.0 215.6 reduce-scatter.1
where the time goes:
time: 471 us; the launch traced here: 469 us
  waiting for transfers between devices  306 us (65%)
  matrix products  92.1 us (20%)
  local copies, waits for them, and re-layouts  26.1 us (6%)
  between operations  14.9 us (3%)
  other arithmetic  14.1 us (3%)
  blocking collectives  11.3 us (2%)
  starting transfers between devices  4.94 us (1%)
    reduce_scatter x1, waiting for transfers between devices, local(): lax.psum_scatter(jnp.dot(window.T, kv_grad, preferred_element_type=jnp.fl...  210 us
    all_gather x1, waiting for transfers between devices, local(): lax.all_gather(columns_full, 'fsdp', axis=0, tiled=True)  95.9 us
    dot_general x4, matrix products, attend(): jnp.einsum('gst,sgd->td', score_low, query_head, preferred_element_type=j...  33.8 us
    unnamed x34, local copies, waits for them, and re-layouts  20.1 us
    sub x4, matrix products, attend(): weights_exp = jnp.exp(scores - top_score)  19.9 us
    all_to_all x1, blocking collectives, copy_for_each(): lax.all_to_all(jnp.broadcast_to(array[None], (devices, *array.shape)), ax...  11.3 us
    dot_general x4, matrix products, attend(): jnp.einsum('sgd,td->gst', grad_head, values_head, preferred_element_type=...  10.8 us
  transfers between devices with their start and end apart: 3, of which 2 were waited for; matrix products, arithmetic and copies ran while one was open for 5% of the time, Pallas kernels for 0%

commit v1 on v0

v1 whole, which is shorter than its diff:
```python
import math

import jax
import jax.numpy as jnp
import numpy as np
from jax import lax
from jax.experimental import pallas as pl
from jax.experimental.pallas import tpu as pltpu
from jax.sharding import PartitionSpec as P

KVH = 4
HD = 128
SEQ = 512
BF = jnp.bfloat16
F32 = jnp.float32
NZ = 8
STEPS = 8
DEPTH = 5
MESH = pl.DeviceIdType.MESH
NT = (((1,), (1,)), ((), ()))
TN = (((0,), (0,)), ((), ()))


def coordinates():
    dp = lax.axis_index("dp")
    fsdp = lax.axis_index("fsdp")
    x = dp // 2
    y = (fsdp // 2) % 2 * 2 + dp % 2
    z = fsdp // 4
    c = fsdp % 2
    return x, y, z, c


def device(x, y, z, c):
    return (x * 2 + y % 2, (z * 2 + y // 2) * 2 + c)


def offset(step):
    return (step + 1) // 2 * (2 * (step % 2) - 1)


class Ring:
    def __init__(self, colour, x, y, z, c):
        self.colour = colour
        self.x, self.y, self.z, self.c = x, y, z, c
        self.p1, self.p2 = (y, x) if colour == 0 else (x, y)

    def along1(self, shift):
        if self.colour == 0:
            return device(self.x, (self.y + shift + 4) % 4, self.z, self.c)
        return device((self.x + shift + 4) % 4, self.y, self.z, self.c)

    def along2(self, shift):
        if self.colour == 0:
            return device((self.x + shift + 4) % 4, self.y, self.z, self.c)
        return device(self.x, (self.y + shift + 4) % 4, self.z, self.c)


def remote(src, dst, send, recv, target):
    return pltpu.make_async_remote_copy(
        src_ref=src, dst_ref=dst, send_sem=send, recv_sem=recv, device_id=target, device_id_type=MESH
    )


def greet(x, y, z, c):
    barrier = pltpu.get_barrier_semaphore()
    peers = [device(x, y, (z + shift) % NZ, c) for shift in range(1, NZ)]
    peers += [device((x + shift) % 4, y, z, c) for shift in (1, 3)]
    peers += [device(x, (y + shift) % 4, z, c) for shift in (1, 3)]
    peers += [device(x, y, z, 1 - c)]
    for peer in peers:
        pl.semaphore_signal(barrier, inc=1, device_id=peer, device_id_type=MESH)
    return barrier, len(peers)


def project_kernel(
    start_ref, mid_ref, end_ref, time_ref, hidden_hbm, out_ref,
    hidden, buf, acc, zs, zr, as_, ar, bs, br, ds_, dr, hsem,
):
    x, y, z, c = coordinates()
    barrier, count = greet(x, y, z, c)
    load = pltpu.make_async_copy(hidden_hbm, hidden, hsem)
    load.start()
    t = time_ref[0]
    blended = (
        (1.0 - t) ** 2 * start_ref[...].astype(F32)
        + 2.0 * t * (1.0 - t) * mid_ref[...].astype(F32)
        + t**2 * end_ref[...].astype(F32)
    ).astype(BF)
    buf[0, z, c, x, y] = blended[:64]
    buf[1, z, c, y, x] = blended[64:]
    acc[...] = jnp.zeros_like(acc)
    rings = [Ring(k, x, y, z, c) for k in range(2)]
    pl.semaphore_wait(barrier, count)

    def zcopy(k, s):
        ring = rings[k]
        block = buf.at[k, z, c, ring.p2, ring.p1]
        return remote(block, block, zs.at[k, s], zr.at[k, s], device(x, y, (z - offset(s) + NZ) % NZ, c))

    def near1(k, s, way):
        ring = rings[k]
        block = buf.at[k, (z + offset(s) + NZ) % NZ, c, ring.p2, ring.p1]
        return remote(block, block, as_.at[k, s, way], ar.at[k, s, way], ring.along1(1 - 2 * way))

    def far1(k, s):
        ring = rings[k]
        shift = 1 - 2 * (s % 2)
        block = buf.at[k, (z + offset(s) + NZ) % NZ, c, ring.p2, (ring.p1 - shift + 4) % 4]
        return remote(block, block, as_.at[k, s, 2], ar.at[k, s, 2], ring.along1(shift))

    def near2(k, s, way):
        ring = rings[k]
        block = buf.at[k, (z + offset(s) + NZ) % NZ, c, ring.p2]
        return remote(block, block, bs.at[k, s, way], br.at[k, s, way], ring.along2(1 - 2 * way))

    def far2(k, s):
        ring = rings[k]
        shift = 1 - 2 * (s % 2)
        block = buf.at[k, (z + offset(s) + NZ) % NZ, c, (ring.p2 - shift + 4) % 4]
        return remote(block, block, bs.at[k, s, 2], br.at[k, s, 2], ring.along2(shift))

    def cross(k, s):
        block = buf.at[k, (z + offset(s) + NZ) % NZ, c]
        return remote(block, block, ds_.at[k, s], dr.at[k, s], device(x, y, z, 1 - c))

    for s in range(1, STEPS):
        for k in range(2):
            zcopy(k, s).start()
    load.wait()

    def body(t, carry):
        @pl.when(t < STEPS)
        def _():
            @pl.when(t > 0)
            def _():
                for k in range(2):
                    zcopy(k, t).wait_recv()

            for k in range(2):
                near1(k, t, 0).start()
                near1(k, t, 1).start()

        @pl.when((t >= 1) & (t < STEPS + 1))
        def _():
            s = t - 1
            for k in range(2):
                near1(k, s, 0).wait_recv()
                near1(k, s, 1).wait_recv()
                far1(k, s).start()

        @pl.when((t >= 2) & (t < STEPS + 2))
        def _():
            s = t - 2
            for k in range(2):
                far1(k, s).wait_recv()
                near2(k, s, 0).start()
                near2(k, s, 1).start()

        @pl.when((t >= 3) & (t < STEPS + 3))
        def _():
            s = t - 3
            for k in range(2):
                near2(k, s, 0).wait_recv()
                near2(k, s, 1).wait_recv()
                far2(k, s).start()

        @pl.when((t >= 4) & (t < STEPS + 4))
        def _():
            s = t - 4
            for k in range(2):
                far2(k, s).wait_recv()
                cross(k, s).start()

        @pl.when(t >= 5)
        def _():
            s = t - 5
            for k in range(2):
                cross(k, s).wait_recv()
            zb = (z + offset(s) + NZ) % NZ
            lhs = hidden[:, pl.ds(pl.multiple_of(zb * 512, 512), 512)]
            for n in range(4):
                groups = []
                for y_hi in range(2):
                    for core in range(2):
                        for k in range(2):
                            parts = []
                            for y_lo in range(2):
                                yy = y_hi * 2 + y_lo
                                place = (n, yy) if k == 0 else (yy, n)
                                parts.append(buf[k, zb, core, place[0], place[1]])
                            groups.append(jnp.concatenate(parts, axis=1))
                rhs = jnp.concatenate(groups, axis=0)
                acc[:, n * 256 : (n + 1) * 256] += jnp.dot(lhs, rhs, preferred_element_type=F32)

        return carry

    lax.fori_loop(0, STEPS + DEPTH, body, 0)
    out_ref[...] = acc[...].astype(BF)

    def drain(s, carry):
        for k in range(2):
            @pl.when(s > 0)
            def _():
                zcopy(k, s).wait_send()

            near1(k, s, 0).wait_send()
            near1(k, s, 1).wait_send()
            far1(k, s).wait_send()
            near2(k, s, 0).wait_send()
            near2(k, s, 1).wait_send()
            far2(k, s).wait_send()
            cross(k, s).wait_send()
        return carry

    lax.fori_loop(0, STEPS, drain, 0)


def project(start, mid, end, time, hidden):
    vmem = pl.BlockSpec(memory_space=pltpu.VMEM)
    dma = pltpu.SemaphoreType.DMA
    return pl.pallas_call(
        project_kernel,
        name="gather_project",
        out_shape=jax.ShapeDtypeStruct((SEQ, 1024), BF),
        in_specs=[vmem, vmem, vmem, pl.BlockSpec(memory_space=pltpu.SMEM), pl.BlockSpec(memory_space=pl.ANY)],
        out_specs=vmem,
        scratch_shapes=[
            pltpu.VMEM((SEQ, 4096), BF),
            pltpu.VMEM((2, NZ, 2, 4, 4, 64, 128), BF),
            pltpu.VMEM((SEQ, 1024), F32),
            dma((2, STEPS)), dma((2, STEPS)),
            dma((2, STEPS, 3)), dma((2, STEPS, 3)),
            dma((2, STEPS, 3)), dma((2, STEPS, 3)),
            dma((2, STEPS)), dma((2, STEPS)),
            dma(()),
        ],
        compiler_params=pltpu.CompilerParams(collective_id=0, has_side_effects=True, vmem_limit_bytes=60 * 2**20),
    )(start, mid, end, time, hidden)


ROWS = 256
SCALE = 1.0 / math.sqrt(HD)
FOLD = SCALE * math.log2(math.e)


def attend_kernel(
    keys_ref, values_ref, query_ref, grad_ref, cos_ref, sin_ref, cost_ref, sint_ref,
    context_ref, key_grad_ref, value_grad_ref, key_acc, value_acc,
):
    raw = keys_ref[...].astype(F32)
    keys = (raw * cos_ref[...] + pltpu.roll(raw, 64, 1) * sin_ref[...]).astype(BF)
    values = values_ref[...]
    key_acc[...] = jnp.zeros_like(key_acc)
    value_acc[...] = jnp.zeros_like(value_acc)
    for tile in range(SEQ // ROWS):
        rows = slice(tile * ROWS, (tile + 1) * ROWS)
        length = (tile + 1) * ROWS
        k_t = keys[:length]
        v_t = values[:length]
        position = lax.broadcasted_iota(jnp.int32, (ROWS, length), 0) + tile * ROWS
        causal = position >= lax.broadcasted_iota(jnp.int32, (ROWS, length), 1)
        for head in range(4):
            columns = slice(head * HD, (head + 1) * HD)
            query = query_ref[rows, columns]
            grad = grad_ref[rows, columns]
            scores = lax.dot_general(query, k_t, NT, preferred_element_type=F32)
            scores = jnp.where(causal, scores, -1e30)
            top = jnp.max(scores, axis=-1, keepdims=True)
            weights = jnp.exp2((scores - top) * FOLD)
            probs = weights * (1.0 / jnp.sum(weights, axis=-1, keepdims=True))
            low = probs.astype(BF)
            context = jnp.dot(low, v_t, preferred_element_type=F32)
            context_ref[rows, columns] = context.astype(BF)
            inner = jnp.sum(context * grad.astype(F32), axis=-1, keepdims=True)
            dprobs = lax.dot_general(grad, v_t, NT, preferred_element_type=F32)
            dscores = (probs * (dprobs - inner)).astype(BF)
            value_acc[:, :length] += lax.dot_general(grad, low, TN, preferred_element_type=F32)
            key_acc[:, :length] += lax.dot_general(query, dscores, TN, preferred_element_type=F32)
    value_grad_ref[...] = value_acc[...].astype(BF)
    first = key_acc[:64] * SCALE
    second = key_acc[64:] * SCALE
    cos = cost_ref[...]
    sin = sint_ref[...]
    key_grad_ref[:64] = (first * cos + second * sin).astype(BF)
    key_grad_ref[64:] = (second * cos - first * sin).astype(BF)


def tables():
    half = HD // 2
    inverse = np.exp(-(2.0 * np.arange(half) / HD) * math.log(500000.0))
    angles = np.arange(SEQ)[:, None] * inverse[None, :]
    cos = np.cos(angles).astype(np.float32)
    sin = np.sin(angles).astype(np.float32)
    return (
        np.concatenate([cos, cos], axis=1),
        np.concatenate([-sin, sin], axis=1),
        np.ascontiguousarray(cos.T),
        np.ascontiguousarray(sin.T),
    )


def attend(kv, queries, cotangent):
    cos, sin, cost, sint = (jnp.asarray(table) for table in tables())
    whole = lambda shape: pl.BlockSpec(shape, lambda j: (0, 0))
    return pl.pallas_call(
        attend_kernel,
        name="attend",
        grid=(KVH,),
        out_shape=(
            jax.ShapeDtypeStruct((SEQ, 2048), BF),
            jax.ShapeDtypeStruct((512, SEQ), BF),
            jax.ShapeDtypeStruct((512, SEQ), BF),
        ),
        in_specs=[
            pl.BlockSpec((SEQ, HD), lambda j: (0, j)),
            pl.BlockSpec((SEQ, HD), lambda j: (0, j + KVH)),
            pl.BlockSpec((SEQ, 512), lambda j: (0, j)),
            pl.BlockSpec((SEQ, 512), lambda j: (0, j)),
            whole((SEQ, HD)), whole((SEQ, HD)), whole((HD // 2, SEQ)), whole((HD // 2, SEQ)),
        ],
        out_specs=(
            pl.BlockSpec((SEQ, 512), lambda j: (0, j)),
            pl.BlockSpec((HD, SEQ), lambda j: (j, 0)),
            pl.BlockSpec((HD, SEQ), lambda j: (j, 0)),
        ),
        scratch_shapes=[pltpu.VMEM((HD, SEQ), F32), pltpu.VMEM((HD, SEQ), F32)],
        compiler_params=pltpu.CompilerParams(vmem_limit_bytes=40 * 2**20),
    )(kv, kv, queries, cotangent, cos, sin, cost, sint)


def reduce_kernel(
    key_ref, value_ref, hidden_hbm, out_ref,
    hidden, dsend, drecv, own, total, far2r, near2r, mid, far1r, near1r, zsend, zrecv, last,
    ds_, dr, bs, br, as_, ar, zs, zr, hsem,
):
    x, y, z, c = coordinates()
    barrier, count = greet(x, y, z, c)
    load = pltpu.make_async_copy(hidden_hbm, hidden, hsem)
    load.start()
    rings = [Ring(k, x, y, z, c) for k in range(2)]

    def target(s):
        return (z + offset(7 - s) + NZ) % NZ

    def cross(k, s):
        return remote(dsend.at[s, k], drecv.at[s, k], ds_.at[k, s], dr.at[k, s], device(x, y, z, 1 - c))

    def far2(k, s):
        ring = rings[k]
        shift = 1 - 2 * (s % 2)
        return remote(
            total.at[s, k, (ring.p2 + 2) % 4], far2r.at[s, k], bs.at[k, s, 2], br.at[k, s, 2], ring.along2(shift)
        )

    def near2(k, s, way):
        ring = rings[k]
        shift = 1 - 2 * way
        return remote(
            total.at[s, k, (ring.p2 + shift + 4) % 4], near2r.at[s, k, way],
            bs.at[k, s, way], br.at[k, s, way], ring.along2(shift),
        )

    def far1(k, s):
        ring = rings[k]
        shift = 1 - 2 * (s % 2)
        return remote(
            mid.at[s, k, (ring.p1 + 2) % 4], far1r.at[s, k], as_.at[k, s, 2], ar.at[k, s, 2], ring.along1(shift)
        )

    def near1(k, s, way):
        ring = rings[k]
        shift = 1 - 2 * way
        return remote(
            mid.at[s, k, (ring.p1 + shift + 4) % 4], near1r.at[s, k, way],
            as_.at[k, s, way], ar.at[k, s, way], ring.along1(shift),
        )

    def zcopy(k, s):
        return remote(zsend.at[s, k], zrecv.at[s, k], zs.at[k, s], zr.at[k, s], device(x, y, target(s), c))

    def product(s, core, store):
        base = target(s) * 512 + core * 128
        rhs = jnp.concatenate(
            [hidden[:, pl.ds(pl.multiple_of(base + y_hi * 256, 128), 128)] for y_hi in range(2)], axis=1
        )
        for part, ref in enumerate((key_ref, value_ref)):
            grads = jnp.dot(ref[...], rhs, preferred_element_type=F32)
            for row in range(4):
                xx = part * 2 + row // 2
                for y_hi in range(2):
                    yy = y_hi * 2 + row % 2
                    lanes = slice(y_hi * 128, (y_hi + 1) * 128)
                    store(0, xx, yy, grads[row * 128 : row * 128 + 64, lanes])
                    store(1, yy, xx, grads[row * 128 + 64 : row * 128 + 128, lanes])

    pl.semaphore_wait(barrier, count)
    load.wait()

    def body(t, carry):
        @pl.when(t >= 5)
        def _():
            s = t - 5
            for k in range(2):
                near1(k, s, 0).wait_recv()
                near1(k, s, 1).wait_recv()
                summed = (
                    mid[s, k, rings[k].p1].astype(F32) + near1r[s, k, 0].astype(F32) + near1r[s, k, 1].astype(F32)
                )
                last[k] = summed
                zsend[s, k] = summed.astype(BF)

                @pl.when(s < STEPS - 1)
                def _():
                    zcopy(k, s).start()

        @pl.when((t >= 4) & (t < STEPS + 4))
        def _():
            s = t - 4
            for k in range(2):
                far1(k, s).wait_recv()
                place = (rings[k].p1 + 1 - 2 * (s % 2) + 4) % 4
                mid[s, k, place] = (mid[s, k, place].astype(F32) + far1r[s, k].astype(F32)).astype(BF)
                near1(k, s, 0).start()
                near1(k, s, 1).start()

        @pl.when((t >= 3) & (t < STEPS + 3))
        def _():
            s = t - 3
            for k in range(2):
                near2(k, s, 0).wait_recv()
                near2(k, s, 1).wait_recv()
                mid[s, k] = (
                    total[s, k, rings[k].p2].astype(F32)
                    + near2r[s, k, 0].astype(F32)
                    + near2r[s, k, 1].astype(F32)
                ).astype(BF)
                far1(k, s).start()

        @pl.when((t >= 2) & (t < STEPS + 2))
        def _():
            s = t - 2
            for k in range(2):
                far2(k, s).wait_recv()
                place = (rings[k].p2 + 1 - 2 * (s % 2) + 4) % 4
                total[s, k, place] = (total[s, k, place].astype(F32) + far2r[s, k].astype(F32)).astype(BF)
                near2(k, s, 0).start()
                near2(k, s, 1).start()

        @pl.when((t >= 1) & (t < STEPS + 1))
        def _():
            s = t - 1
            for k in range(2):
                cross(k, s).wait_recv()
                for place in range(4):
                    total[s, k, place] = (own[k, place] + drecv[s, k, place].astype(F32)).astype(BF)
                far2(k, s).start()

        @pl.when(t < STEPS)
        def _():
            def away(k, i, j, block):
                dsend[t, k, i, j] = block.astype(BF)

            def keep(k, i, j, block):
                own[k, i, j] = block

            product(t, 1 - c, away)
            for k in range(2):
                cross(k, t).start()
            product(t, c, keep)

        return carry

    lax.fori_loop(0, STEPS + DEPTH, body, 0)
    sums = []
    for k in range(2):
        value = last[k]
        for s in range(STEPS - 1):
            zcopy(k, s).wait_recv()
            value = value + zrecv[s, k].astype(F32)
        sums.append(value)
    out_ref[...] = jnp.concatenate(sums, axis=0).T

    def drain(s, carry):
        for k in range(2):
            @pl.when(s < STEPS - 1)
            def _():
                zcopy(k, s).wait_send()

            near1(k, s, 0).wait_send()
            near1(k, s, 1).wait_send()
            far1(k, s).wait_send()
            near2(k, s, 0).wait_send()
            near2(k, s, 1).wait_send()
            far2(k, s).wait_send()
            cross(k, s).wait_send()
        return carry

    lax.fori_loop(0, STEPS, drain, 0)


def reduce(key_grad, value_grad, hidden):
    vmem = pl.BlockSpec(memory_space=pltpu.VMEM)
    dma = pltpu.SemaphoreType.DMA
    return pl.pallas_call(
        reduce_kernel,
        name="gradient_reduce",
        out_shape=jax.ShapeDtypeStruct((128, 128), F32),
        in_specs=[vmem, vmem, pl.BlockSpec(memory_space=pl.ANY)],
        out_specs=vmem,
        scratch_shapes=[
            pltpu.VMEM((SEQ, 4096), BF),
            pltpu.VMEM((STEPS, 2, 4, 4, 64, 128), BF),
            pltpu.VMEM((STEPS, 2, 4, 4, 64, 128), BF),
            pltpu.VMEM((2, 4, 4, 64, 128), F32),
            pltpu.VMEM((STEPS, 2, 4, 4, 64, 128), BF),
            pltpu.VMEM((STEPS, 2, 4, 64, 128), BF),
            pltpu.VMEM((STEPS, 2, 2, 4, 64, 128), BF),
            pltpu.VMEM((STEPS, 2, 4, 64, 128), BF),
            pltpu.VMEM((STEPS, 2, 64, 128), BF),
            pltpu.VMEM((STEPS, 2, 2, 64, 128), BF),
            pltpu.VMEM((STEPS, 2, 64, 128), BF),
            pltpu.VMEM((STEPS, 2, 64, 128), BF),
            pltpu.VMEM((2, 64, 128), F32),
            dma((2, STEPS)), dma((2, STEPS)),
            dma((2, STEPS, 3)), dma((2, STEPS, 3)),
            dma((2, STEPS, 3)), dma((2, STEPS, 3)),
            dma((2, STEPS)), dma((2, STEPS)),
            dma(()),
        ],
        compiler_params=pltpu.CompilerParams(collective_id=1, has_side_effects=True, vmem_limit_bytes=60 * 2**20),
    )(key_grad, value_grad, hidden)


def local(hidden, queries, cotangent, point_start, point_mid, point_end, curve_time):
    kv = project(point_start, point_mid, point_end, curve_time, hidden)
    context, key_grad, value_grad = attend(kv, queries, cotangent)
    gradient = reduce(key_grad, value_grad, hidden)
    t_value = curve_time[0]
    return (context, gradient * (2.0 * t_value * (1.0 - t_value)))


def solution(mesh):
    return jax.shard_map(
        local,
        mesh=mesh,
        in_specs=(
            P(("dp", "fsdp"), None),
            P(("dp", "fsdp"), None),
            P(("dp", "fsdp"), None),
            P("fsdp", "dp"),
            P("fsdp", "dp"),
            P("fsdp", "dp"),
            P(),
        ),
        out_specs=(P(("dp", "fsdp"), None), P("fsdp", "dp")),
        check_vma=False,
    )
```

time: 471 us -> 139 us (0.30)
  waiting for transfers between devices: 306 us -> 0 us
  Pallas kernels: 0 us -> 131 us
  matrix products: 92.1 us -> 0 us
  local copies, waits for them, and re-layouts: 26.1 us -> 4.42 us
  between operations: 14.9 us -> 1.39 us
  other arithmetic: 14.1 us -> 1.48 us
  blocking collectives: 11.3 us -> 0 us
  starting transfers between devices: 4.94 us -> 0 us
    reduce_scatter x1 -> x0, waiting for transfers between devices: 210 us -> none  [local(): lax.psum_scatter(jnp.dot(window.T, kv_grad, preferred_element_type=jnp.fl...]
    pallas_call x0 -> x3, Pallas kernels: none -> 131 us  [the longest x1 58.3 us: reduce(): pl.pallas_call(reduce_kernel, name='gradient_reduce', out_shape=jax.Shape...]
    all_gather x1 -> x0, waiting for transfers between devices: 95.9 us -> none  [local(): lax.all_gather(columns_full, 'fsdp', axis=0, tiled=True)]
    dot_general x18 -> x0, matrix products: 72.2 us -> none  [the longest x4 33.8 us: attend(): jnp.einsum('gst,sgd->td', score_low, query_head, preferred_element_type=j...]
    sub x4 -> x0, matrix products: 19.9 us -> none  [attend(): weights_exp = jnp.exp(scores - top_score)]
    unnamed x34 -> x18, local copies, waits for them, and re-layouts: 20.1 us -> 4.42 us
    all_to_all x1 -> x0, blocking collectives: 11.3 us -> none  [copy_for_each(): lax.all_to_all(jnp.broadcast_to(array[None], (devices, *array.shape)), ax...]
    all_to_all x1 -> x0, starting transfers between devices: 4.86 us -> none  [summed_on_arrival(): lax.all_to_all(in_blocks(array, dim, devices), axis, 0, 0, tiled=True)]
  transfers between devices with their start and end apart: 3 -> 0, of which waited for: 2 -> 0; matrix products, arithmetic and copies ran while one was open for 5% -> 0% of each run, Pallas kernels for 0% -> 0%
where the time goes in v1:
time: 139 us; the launch traced here: 138 us
  Pallas kernels  131 us (94%)
  local copies, waits for them, and re-layouts  4.42 us (3%)
  other arithmetic  1.48 us (1%)
    pallas_call x1, Pallas kernels, reduce(): pl.pallas_call(reduce_kernel, name='gradient_reduce', out_shape=jax.Shape...  58.3 us
    pallas_call x1, Pallas kernels, project(): pl.pallas_call(project_kernel, name='gather_project', out_shape=jax.Shape...  51.7 us
    pallas_call x1, Pallas kernels, attend(): pl.pallas_call(attend_kernel, name='attend', grid=(KVH,), out_shape=(jax....  20.6 us
    unnamed x18, local copies, waits for them, and re-layouts  4.42 us

profile of v1, /device:TPU:2, one launch (start us, length us, event | category | flops | bytes accessed | tf_op | source)
XLA Modules:
  0.0 137.9 jit_solution(8083230335319628086)
XLA Ops:
  1.3 0.0 copy-start.1
  1.3 0.0 copy-start.5
  1.3 0.0 copy-start.6
  1.3 0.0 copy-start.7
  1.3 0.0 copy-start.8
  1.3 51.7 %gather_project.1.keys_ref.values_ref = bf16[512,1024]{1,0:T(8,128)(2,1)} custom-call(bf16[128,128]{1,0:T(8,128)(2,1)} %start_ref.1, bf16[128,128]{1,0:T(8,128)(2,1)} %mid_ref.1, bf16[128,128]{1,0:T(8,128)(2,1)} %end_ref.1, f32[1]{0:T(128)S(6)} %copy.13.time_ref, bf16[512,4096]{1,0:T(8,128)(2,1)} %hidden_hbm.3), custom_call_target="tpu_custom_call" | custom-call | tf_op jit(solution)/shard_map/gather_project/pallas_call | solution.py:222
  53.0 0.0 copy-done.1
  53.0 0.0 copy-done.5
  53.0 0.0 copy-done.6
  53.1 0.0 copy-done.7
  53.1 0.0 copy-done.8
  53.1 0.0 copy-start
  53.1 1.2 copy-done
  54.3 0.0 copy-start.2
  54.3 1.6 %copy-done.2 = bf16[512,2048]{1,0:T(8,128)(2,1)S(1)} copy-done((bf16[512,2048]{1,0:T(8,128)(2,1)S(1)}, bf16[512,2048]{1,0:T(8,128)(2,1)}, u32[]{:S(2)}) %copy-start.2) | copy-done | bytes 2097176
  55.9 20.6 %attend.1 = (bf16[512,2048]{1,0:T(8,128)(2,1)}, bf16[512,512]{1,0:T(8,128)(2,1)S(1)}, bf16[512,512]{1,0:T(8,128)(2,1)S(1)}) custom-call(bf16[512,1024]{1,0:T(8,128)(2,1)S(1)} %copy-done, bf16[512,1024]{1,0:T(8,128)(2,1)S(1)} %copy-done, bf16[512,2048]{1,0:T(8,128)(2,1)S(1)} %copy-done.1, bf16[512,2048]{1,0:T(8,128)(2,1)S(1)} %copy-done.2, ...), custom_call_target="tpu_custom_call" | custom-call | tf_op jit(solution)/shard_map/attend/pallas_call | solution.py:306
  76.5 0.0 copy-start.3
  76.5 0.8 copy-done.3
  77.3 0.0 copy-start.4
  77.3 0.8 copy-done.4
  78.1 58.3 %gradient_reduce.1 = f32[128,128]{1,0:T(8,128)} custom-call(bf16[512,512]{1,0:T(8,128)(2,1)} %copy-done.3, bf16[512,512]{1,0:T(8,128)(2,1)} %copy-done.4, bf16[512,4096]{1,0:T(8,128)(2,1)} %hidden_hbm.3), custom_call_target="tpu_custom_call" | custom-call | tf_op jit(solution)/shard_map/gradient_reduce/pallas_call | solution.py:505
  136.4 1.5 %broadcast_multiply_fusion = f32[128,128]{1,0:T(8,128)} fusion(f32[128,128]{1,0:T(8,128)} %gradient_reduce.1, f32[]{:T(128)} %bitcast), kind=kLoop, calls=%fused_computation | loop fusion | flops 16384 | bytes 131076 | tf_op jit(solution)/shard_map/mul | solution.py:540
Async XLA Ops:
  1.3 51.7 %copy-start.1 = (bf16[512,2048]{1,0:T(8,128)(2,1)S(1)}, bf16[512,2048]{1,0:T(8,128)(2,1)}, u32[]{:S(2)}) copy-start(bf16[512,2048]{1,0:T(8,128)(2,1)} %query_ref.1) | copy-start | bytes 6291460
  1.3 51.7 %copy-start.5 = (f32[512,128]{1,0:T(8,128)S(1)}, f32[512,128]{1,0:T(8,128)}, u32[]{:S(2)}) copy-start(f32[512,128]{1,0:T(8,128)} %constant.15.clone.sin_ref) | copy-start | bytes 786436
  1.3 51.7 %copy-start.6 = (f32[512,128]{1,0:T(8,128)S(1)}, f32[512,128]{1,0:T(8,128)}, u32[]{:S(2)}) copy-start(f32[512,128]{1,0:T(8,128)} %constant.14.clone.cos_ref) | copy-start | bytes 786436
  1.3 51.7 %copy-start.7 = (f32[64,512]{1,0:T(8,128)S(1)}, f32[64,512]{1,0:T(8,128)}, u32[]{:S(2)}) copy-start(f32[64,512]{1,0:T(8,128)} %constant.17.clone.sint_ref) | copy-start | bytes 393220
  1.3 51.7 %copy-start.8 = (f32[64,512]{1,0:T(8,128)S(1)}, f32[64,512]{1,0:T(8,128)}, u32[]{:S(2)}) copy-start(f32[64,512]{1,0:T(8,128)} %constant.16.clone.cost_ref) | copy-start | bytes 393220
  53.1 1.2 copy-start
  54.3 1.6 %copy-start.2 = (bf16[512,2048]{1,0:T(8,128)(2,1)S(1)}, bf16[512,2048]{1,0:T(8,128)(2,1)}, u32[]{:S(2)}) copy-start(bf16[512,2048]{1,0:T(8,128)(2,1)} %grad_ref.1) | copy-start | bytes 6291460
  76.5 0.8 copy-start.3
  77.3 0.8 copy-start.4

commit v2 on v1

v2 whole, which is shorter than its diff:
```python
import math

import jax
import jax.numpy as jnp
import numpy as np
from jax import lax
from jax.experimental import pallas as pl
from jax.experimental.pallas import tpu as pltpu
from jax.sharding import PartitionSpec as P

KVH = 4
HD = 128
SEQ = 512
BF = jnp.bfloat16
F32 = jnp.float32
NZ = 8
STEPS = 8
GATHER = (0, 2, 4, 6, 7)
REDUCE = (0, 1, 3, 6, 9)
MESH = pl.DeviceIdType.MESH
NT = (((1,), (1,)), ((), ()))
TN = (((0,), (0,)), ((), ()))


def coordinates():
    dp = lax.axis_index("dp")
    fsdp = lax.axis_index("fsdp")
    x = dp // 2
    y = (fsdp // 2) % 2 * 2 + dp % 2
    z = fsdp // 4
    c = fsdp % 2
    return x, y, z, c


def device(x, y, z, c):
    return (x * 2 + y % 2, (z * 2 + y // 2) * 2 + c)


def offset(step):
    return (step + 1) // 2 * (2 * (step % 2) - 1)


class Ring:
    def __init__(self, colour, x, y, z, c):
        self.colour = colour
        self.x, self.y, self.z, self.c = x, y, z, c
        self.p1, self.p2 = (y, x) if colour == 0 else (x, y)

    def along1(self, shift):
        if self.colour == 0:
            return device(self.x, (self.y + shift + 4) % 4, self.z, self.c)
        return device((self.x + shift + 4) % 4, self.y, self.z, self.c)

    def along2(self, shift):
        if self.colour == 0:
            return device((self.x + shift + 4) % 4, self.y, self.z, self.c)
        return device(self.x, (self.y + shift + 4) % 4, self.z, self.c)


def remote(src, dst, send, recv, target):
    return pltpu.make_async_remote_copy(
        src_ref=src, dst_ref=dst, send_sem=send, recv_sem=recv, device_id=target, device_id_type=MESH
    )


def greet(x, y, z, c, shifts):
    barrier = pltpu.get_barrier_semaphore()
    peers = [device(x, y, (z + shift) % NZ, c) for shift in shifts]
    peers += [device((x + shift) % 4, y, z, c) for shift in (1, 2, 3)]
    peers += [device(x, (y + shift) % 4, z, c) for shift in (1, 2, 3)]
    peers += [device(x, y, z, 1 - c)]
    for peer in peers:
        pl.semaphore_signal(barrier, inc=1, device_id=peer, device_id_type=MESH)
    return barrier, len(peers)


def pipeline(stages, starts, order):
    def body(t, carry):
        for i in order:
            @pl.when((t >= starts[i]) & (t < STEPS + starts[i]))
            def _():
                stages[i](t - starts[i])

        return carry

    lax.fori_loop(0, STEPS + starts[-1], body, 0)


def project_kernel(
    start_ref, mid_ref, end_ref, time_ref, hidden_hbm, out_ref,
    hidden, buf, acc, zs, zr, as_, ar, bs, br, ds_, dr, hsem,
):
    x, y, z, c = coordinates()
    barrier, count = greet(x, y, z, c, (1, NZ - 1))
    load = pltpu.make_async_copy(hidden_hbm, hidden, hsem)
    load.start()
    t = time_ref[0]
    blended = (
        (1.0 - t) ** 2 * start_ref[...].astype(F32)
        + 2.0 * t * (1.0 - t) * mid_ref[...].astype(F32)
        + t**2 * end_ref[...].astype(F32)
    ).astype(BF)
    buf[0, z, c, x, y] = blended[:64]
    buf[1, z, c, y, x] = blended[64:]
    acc[...] = jnp.zeros_like(acc)
    rings = [Ring(k, x, y, z, c) for k in range(2)]
    pl.semaphore_wait(barrier, count)

    def zblock(s):
        return (z + offset(s) + NZ) % NZ

    def zcopy(k, s):
        sign = 2 * (s % 2) - 1
        block = buf.at[k, (z + offset(s) - sign + NZ) % NZ, c, rings[k].p2, rings[k].p1]
        return remote(block, block, zs.at[k, s], zr.at[k, s], device(x, y, (z - sign + NZ) % NZ, c))

    def first(k, s):
        block = buf.at[k, zblock(s), c, rings[k].p2, rings[k].p1]
        return [
            remote(block, block, as_.at[k, s, i], ar.at[k, s, i], rings[k].along1(shift))
            for i, shift in enumerate((1, -1, 2))
        ]

    def near(k, s):
        block = buf.at[k, zblock(s), c, rings[k].p2]
        return [
            remote(block, block, bs.at[k, s, i], br.at[k, s, i], rings[k].along2(shift))
            for i, shift in enumerate((1, -1))
        ]

    def far(k, s):
        copies = []
        for i, shift in enumerate((1, -1)):
            block = buf.at[k, zblock(s), c, (rings[k].p2 - shift + 4) % 4, pl.ds(2 * i, 2)]
            copies.append(remote(block, block, bs.at[k, s, 2 + i], br.at[k, s, 2 + i], rings[k].along2(shift)))
        return copies

    def cross(k, s):
        block = buf.at[k, zblock(s), c]
        return remote(block, block, ds_.at[k, s], dr.at[k, s], device(x, y, z, 1 - c))

    for s in range(1, 3):
        for k in range(2):
            zcopy(k, s).start()
    load.wait()

    def stage0(s):
        @pl.when(s > 0)
        def _():
            for k in range(2):
                zcopy(k, s).wait_recv()

            @pl.when(s < STEPS - 2)
            def _():
                for k in range(2):
                    zcopy(k, s + 2).start()

        for k in range(2):
            for copy in first(k, s):
                copy.start()

    def stage1(s):
        for k in range(2):
            for copy in first(k, s):
                copy.wait_recv()
            for copy in near(k, s):
                copy.start()

    def stage2(s):
        for k in range(2):
            for copy in near(k, s):
                copy.wait_recv()
            for copy in far(k, s):
                copy.start()

    def stage3(s):
        for k in range(2):
            for copy in far(k, s):
                copy.wait_recv()
            cross(k, s).start()

    def stage4(s):
        for k in range(2):
            cross(k, s).wait_recv()
        zb = zblock(s)
        lhs = hidden[:, pl.ds(pl.multiple_of(zb * 512, 512), 512)]
        for n in range(4):
            groups = []
            for y_hi in range(2):
                for core in range(2):
                    for k in range(2):
                        parts = []
                        for y_lo in range(2):
                            yy = y_hi * 2 + y_lo
                            place = (n, yy) if k == 0 else (yy, n)
                            parts.append(buf[k, zb, core, place[0], place[1]])
                        groups.append(jnp.concatenate(parts, axis=1))
            rhs = jnp.concatenate(groups, axis=0)
            acc[:, n * 256 : (n + 1) * 256] += jnp.dot(lhs, rhs, preferred_element_type=F32)

    pipeline((stage0, stage1, stage2, stage3, stage4), GATHER, range(5))
    out_ref[...] = acc[...].astype(BF)

    def drain(s, carry):
        for k in range(2):
            @pl.when(s > 0)
            def _():
                zcopy(k, s).wait_send()

            for copy in first(k, s) + near(k, s) + far(k, s) + [cross(k, s)]:
                copy.wait_send()
        return carry

    lax.fori_loop(0, STEPS, drain, 0)


def project(start, mid, end, time, hidden):
    vmem = pl.BlockSpec(memory_space=pltpu.VMEM)
    dma = pltpu.SemaphoreType.DMA
    return pl.pallas_call(
        project_kernel,
        name="gather_project",
        out_shape=jax.ShapeDtypeStruct((SEQ, 1024), BF),
        in_specs=[vmem, vmem, vmem, pl.BlockSpec(memory_space=pltpu.SMEM), pl.BlockSpec(memory_space=pl.ANY)],
        out_specs=vmem,
        scratch_shapes=[
            pltpu.VMEM((SEQ, 4096), BF),
            pltpu.VMEM((2, NZ, 2, 4, 4, 64, 128), BF),
            pltpu.VMEM((SEQ, 1024), F32),
            dma((2, STEPS)), dma((2, STEPS)),
            dma((2, STEPS, 3)), dma((2, STEPS, 3)),
            dma((2, STEPS, 4)), dma((2, STEPS, 4)),
            dma((2, STEPS)), dma((2, STEPS)),
            dma(()),
        ],
        compiler_params=pltpu.CompilerParams(collective_id=0, has_side_effects=True, vmem_limit_bytes=60 * 2**20),
    )(start, mid, end, time, hidden)


ROWS = 256
SCALE = 1.0 / math.sqrt(HD)
FOLD = SCALE * math.log2(math.e)


def attend_kernel(
    keys_ref, values_ref, query_ref, grad_ref, cos_ref, sin_ref, cost_ref, sint_ref,
    context_ref, key_grad_ref, value_grad_ref, key_acc, value_acc,
):
    raw = keys_ref[...].astype(F32)
    keys = (raw * cos_ref[...] + pltpu.roll(raw, 64, 1) * sin_ref[...]).astype(BF)
    values = values_ref[...]
    key_acc[...] = jnp.zeros_like(key_acc)
    value_acc[...] = jnp.zeros_like(value_acc)
    causal = lax.broadcasted_iota(jnp.int32, (ROWS, ROWS), 0) >= lax.broadcasted_iota(jnp.int32, (ROWS, ROWS), 1)
    causal = jnp.concatenate([causal] * 4, axis=0)
    for tile in range(SEQ // ROWS):
        rows = slice(tile * ROWS, (tile + 1) * ROWS)
        length = (tile + 1) * ROWS
        k_t = keys[:length]
        v_t = values[:length]
        query = jnp.concatenate([query_ref[rows, h * HD : (h + 1) * HD] for h in range(4)], axis=0)
        grad = jnp.concatenate([grad_ref[rows, h * HD : (h + 1) * HD] for h in range(4)], axis=0)
        scores = lax.dot_general(query, k_t, NT, preferred_element_type=F32)
        dprobs = lax.dot_general(grad, v_t, NT, preferred_element_type=F32)
        diagonal = jnp.where(causal, scores[:, length - ROWS :], -1e30)
        scores = diagonal if tile == 0 else jnp.concatenate([scores[:, : length - ROWS], diagonal], axis=1)
        top = jnp.max(scores, axis=-1, keepdims=True)
        weights = jnp.exp2((scores - top) * FOLD)
        probs = weights * (1.0 / jnp.sum(weights, axis=-1, keepdims=True))
        low = probs.astype(BF)
        context = jnp.dot(low, v_t, preferred_element_type=F32)
        for h in range(4):
            context_ref[rows, h * HD : (h + 1) * HD] = context[h * ROWS : (h + 1) * ROWS].astype(BF)
        inner = jnp.sum(context * grad.astype(F32), axis=-1, keepdims=True)
        dscores = (probs * (dprobs - inner)).astype(BF)
        value_acc[:, :length] += lax.dot_general(grad, low, TN, preferred_element_type=F32)
        key_acc[:, :length] += lax.dot_general(query, dscores, TN, preferred_element_type=F32)
    value_grad_ref[...] = value_acc[...].astype(BF)
    first = key_acc[:64] * SCALE
    second = key_acc[64:] * SCALE
    cos = cost_ref[...]
    sin = sint_ref[...]
    key_grad_ref[:64] = (first * cos + second * sin).astype(BF)
    key_grad_ref[64:] = (second * cos - first * sin).astype(BF)


def tables():
    half = HD // 2
    inverse = np.exp(-(2.0 * np.arange(half) / HD) * math.log(500000.0))
    angles = np.arange(SEQ)[:, None] * inverse[None, :]
    cos = np.cos(angles).astype(np.float32)
    sin = np.sin(angles).astype(np.float32)
    return (
        np.concatenate([cos, cos], axis=1),
        np.concatenate([-sin, sin], axis=1),
        np.ascontiguousarray(cos.T),
        np.ascontiguousarray(sin.T),
    )


def attend(kv, queries, cotangent):
    cos, sin, cost, sint = (jnp.asarray(table) for table in tables())
    whole = lambda shape: pl.BlockSpec(shape, lambda j: (0, 0))
    return pl.pallas_call(
        attend_kernel,
        name="attend",
        grid=(KVH,),
        out_shape=(
            jax.ShapeDtypeStruct((SEQ, 2048), BF),
            jax.ShapeDtypeStruct((512, SEQ), BF),
            jax.ShapeDtypeStruct((512, SEQ), BF),
        ),
        in_specs=[
            pl.BlockSpec((SEQ, HD), lambda j: (0, j)),
            pl.BlockSpec((SEQ, HD), lambda j: (0, j + KVH)),
            pl.BlockSpec((SEQ, 512), lambda j: (0, j)),
            pl.BlockSpec((SEQ, 512), lambda j: (0, j)),
            whole((SEQ, HD)), whole((SEQ, HD)), whole((HD // 2, SEQ)), whole((HD // 2, SEQ)),
        ],
        out_specs=(
            pl.BlockSpec((SEQ, 512), lambda j: (0, j)),
            pl.BlockSpec((HD, SEQ), lambda j: (j, 0)),
            pl.BlockSpec((HD, SEQ), lambda j: (j, 0)),
        ),
        scratch_shapes=[pltpu.VMEM((HD, SEQ), F32), pltpu.VMEM((HD, SEQ), F32)],
        compiler_params=pltpu.CompilerParams(vmem_limit_bytes=60 * 2**20),
    )(kv, kv, queries, cotangent, cos, sin, cost, sint)


def reduce_kernel(
    key_ref, value_ref, hidden_hbm, out_ref,
    hidden, dsend, drecv, own, total, farr, nearr, mid, firstr, zsend, zrecv, last,
    ds_, dr, bs, br, as_, ar, zs, zr, hsem,
):
    x, y, z, c = coordinates()
    barrier, count = greet(x, y, z, c, range(1, NZ))
    load = pltpu.make_async_copy(hidden_hbm, hidden, hsem)
    load.start()
    rings = [Ring(k, x, y, z, c) for k in range(2)]

    def target(s):
        return (z + offset(7 - s) + NZ) % NZ

    def cross(k, s):
        return remote(dsend.at[s, k], drecv.at[s, k], ds_.at[k, s], dr.at[k, s], device(x, y, z, 1 - c))

    def far(k, s):
        copies = []
        for i, shift in enumerate((1, -1)):
            half = pl.ds(2 * i, 2)
            source = total.at[s, k, (rings[k].p2 + 2) % 4, half]
            copies.append(
                remote(source, farr.at[s, k, half], bs.at[k, s, 2 + i], br.at[k, s, 2 + i], rings[k].along2(shift))
            )
        return copies

    def near(k, s):
        return [
            remote(
                total.at[s, k, (rings[k].p2 + shift + 4) % 4], nearr.at[s, k, i],
                bs.at[k, s, i], br.at[k, s, i], rings[k].along2(shift),
            )
            for i, shift in enumerate((1, -1))
        ]

    def first(k, s):
        return [
            remote(
                mid.at[s, k, (rings[k].p1 + shift + 4) % 4], firstr.at[s, k, i],
                as_.at[k, s, i], ar.at[k, s, i], rings[k].along1(shift),
            )
            for i, shift in enumerate((1, -1, 2))
        ]

    def zcopy(k, s):
        return remote(zsend.at[s, k], zrecv.at[s, k], zs.at[k, s], zr.at[k, s], device(x, y, target(s), c))

    def product(s, core, store):
        base = target(s) * 512 + core * 128
        rhs = jnp.concatenate(
            [hidden[:, pl.ds(pl.multiple_of(base + y_hi * 256, 128), 128)] for y_hi in range(2)], axis=1
        )
        for part, ref in enumerate((key_ref, value_ref)):
            grads = jnp.dot(ref[...], rhs, preferred_element_type=F32)
            for row in range(4):
                xx = part * 2 + row // 2
                for y_hi in range(2):
                    yy = y_hi * 2 + row % 2
                    lanes = slice(y_hi * 128, (y_hi + 1) * 128)
                    store(0, xx, yy, grads[row * 128 : row * 128 + 64, lanes])
                    store(1, yy, xx, grads[row * 128 + 64 : row * 128 + 128, lanes])

    def give(s):
        def away(k, i, j, block):
            dsend[s, k, i, j] = block.astype(BF)

        product(s, 1 - c, away)

    def stage0(s):
        def keep(k, i, j, block):
            own[s % 4, k, i, j] = block

        @pl.when(s > 0)
        def _():
            give(s)

        for k in range(2):
            cross(k, s).start()
        product(s, c, keep)

    def stage1(s):
        for k in range(2):
            cross(k, s).wait_recv()
            for place in range(4):
                total[s, k, place] = (own[s % 4, k, place] + drecv[s, k, place].astype(F32)).astype(BF)
            for copy in far(k, s):
                copy.start()

    def stage2(s):
        for k in range(2):
            for copy in far(k, s):
                copy.wait_recv()
            for i, shift in enumerate((1, -1)):
                place = (rings[k].p2 + shift + 4) % 4
                half = slice(2 * i, 2 * i + 2)
                total[s, k, place, half] = (
                    total[s, k, place, half].astype(F32) + farr[s, k, half].astype(F32)
                ).astype(BF)
            for copy in near(k, s):
                copy.start()

    def stage3(s):
        for k in range(2):
            for copy in near(k, s):
                copy.wait_recv()
            mid[s, k] = (
                total[s, k, rings[k].p2].astype(F32) + nearr[s, k, 0].astype(F32) + nearr[s, k, 1].astype(F32)
            ).astype(BF)
            for copy in first(k, s):
                copy.start()

    def stage4(s):
        for k in range(2):
            for copy in first(k, s):
                copy.wait_recv()
            summed = mid[s, k, rings[k].p1].astype(F32)
            for i in range(3):
                summed = summed + firstr[s, k, i].astype(F32)
            last[k] = summed
            zsend[s, k] = summed.astype(BF)

        @pl.when(s < STEPS - 1)
        def _():
            for k in range(2):
                zcopy(k, s).start()

    load.wait()
    give(0)
    pl.semaphore_wait(barrier, count)
    pipeline((stage0, stage1, stage2, stage3, stage4), REDUCE, (2, 1, 3, 4, 0))
    sums = []
    for k in range(2):
        value = last[k]
        for s in range(STEPS - 1):
            zcopy(k, s).wait_recv()
            value = value + zrecv[s, k].astype(F32)
        sums.append(value)
    out_ref[...] = jnp.concatenate(sums, axis=0).T

    def drain(s, carry):
        for k in range(2):
            @pl.when(s < STEPS - 1)
            def _():
                zcopy(k, s).wait_send()

            for copy in first(k, s) + near(k, s) + far(k, s) + [cross(k, s)]:
                copy.wait_send()
        return carry

    lax.fori_loop(0, STEPS, drain, 0)


def reduce(key_grad, value_grad, hidden):
    vmem = pl.BlockSpec(memory_space=pltpu.VMEM)
    dma = pltpu.SemaphoreType.DMA
    return pl.pallas_call(
        reduce_kernel,
        name="gradient_reduce",
        out_shape=jax.ShapeDtypeStruct((128, 128), F32),
        in_specs=[vmem, vmem, pl.BlockSpec(memory_space=pl.ANY)],
        out_specs=vmem,
        scratch_shapes=[
            pltpu.VMEM((SEQ, 4096), BF),
            pltpu.VMEM((STEPS, 2, 4, 4, 64, 128), BF),
            pltpu.VMEM((STEPS, 2, 4, 4, 64, 128), BF),
            pltpu.VMEM((4, 2, 4, 4, 64, 128), F32),
            pltpu.VMEM((STEPS, 2, 4, 4, 64, 128), BF),
            pltpu.VMEM((STEPS, 2, 4, 64, 128), BF),
            pltpu.VMEM((STEPS, 2, 2, 4, 64, 128), BF),
            pltpu.VMEM((STEPS, 2, 4, 64, 128), BF),
            pltpu.VMEM((STEPS, 2, 3, 64, 128), BF),
            pltpu.VMEM((STEPS, 2, 64, 128), BF),
            pltpu.VMEM((STEPS, 2, 64, 128), BF),
            pltpu.VMEM((2, 64, 128), F32),
            dma((2, STEPS)), dma((2, STEPS)),
            dma((2, STEPS, 4)), dma((2, STEPS, 4)),
            dma((2, STEPS, 3)), dma((2, STEPS, 3)),
            dma((2, STEPS)), dma((2, STEPS)),
            dma(()),
        ],
        compiler_params=pltpu.CompilerParams(collective_id=1, has_side_effects=True, vmem_limit_bytes=60 * 2**20),
    )(key_grad, value_grad, hidden)


def local(hidden, queries, cotangent, point_start, point_mid, point_end, curve_time):
    kv = project(point_start, point_mid, point_end, curve_time, hidden)
    context, key_grad, value_grad = attend(kv, queries, cotangent)
    gradient = reduce(key_grad, value_grad, hidden)
    t_value = curve_time[0]
    return (context, gradient * (2.0 * t_value * (1.0 - t_value)))


def solution(mesh):
    return jax.shard_map(
        local,
        mesh=mesh,
        in_specs=(
            P(("dp", "fsdp"), None),
            P(("dp", "fsdp"), None),
            P(("dp", "fsdp"), None),
            P("fsdp", "dp"),
            P("fsdp", "dp"),
            P("fsdp", "dp"),
            P(),
        ),
        out_specs=(P(("dp", "fsdp"), None), P("fsdp", "dp")),
        check_vma=False,
    )
```

time: 139 us -> 101 us (0.73)
  Pallas kernels: 131 us -> 98.1 us
  local copies, waits for them, and re-layouts: 4.42 us -> 0 us
    pallas_call x1, Pallas kernels: 58.3 us -> 42.2 us  [reduce(): pl.pallas_call(reduce_kernel, name='gradient_reduce', out_shape=jax.Shape...]
    pallas_call x1, Pallas kernels: 51.7 us -> 42.1 us  [project(): pl.pallas_call(project_kernel, name='gather_project', out_shape=jax.Shape...]
    pallas_call x1, Pallas kernels: 20.6 us -> 13.8 us  [attend(): pl.pallas_call(attend_kernel, name='attend', grid=(KVH,), out_shape=(jax....]
    unnamed x18 -> x0, local copies, waits for them, and re-layouts: 4.42 us -> none
where the time goes in v2:
time: 101 us
  Pallas kernels  98.1 us (97%)
  other arithmetic  1.48 us (1%)
  between operations  1.3 us (1%)
    pallas_call x1, Pallas kernels, reduce(): pl.pallas_call(reduce_kernel, name='gradient_reduce', out_shape=jax.Shape...  42.2 us
    pallas_call x1, Pallas kernels, project(): pl.pallas_call(project_kernel, name='gather_project', out_shape=jax.Shape...  42.1 us
    pallas_call x1, Pallas kernels, attend(): pl.pallas_call(attend_kernel, name='attend', grid=(KVH,), out_shape=(jax....  13.8 us

profile of v2, /device:TPU:2, one launch (start us, length us, event | category | flops | bytes accessed | tf_op | source)
XLA Modules:
  0.0 100.9 jit_solution(5424455648490303440)
XLA Ops:
  1.3 42.1 %gather_project.1.keys_ref.values_ref = bf16[512,1024]{1,0:T(8,128)(2,1)} custom-call(bf16[128,128]{1,0:T(8,128)(2,1)} %start_ref.1, bf16[128,128]{1,0:T(8,128)(2,1)} %mid_ref.1, bf16[128,128]{1,0:T(8,128)(2,1)} %end_ref.1, f32[1]{0:T(128)S(6)} %copy.13.time_ref, bf16[512,4096]{1,0:T(8,128)(2,1)} %hidden_hbm.3), custom_call_target="tpu_custom_call" | custom-call | tf_op jit(solution)/shard_map/gather_project/pallas_call | solution.py:220
  43.3 13.8 %attend.1 = (bf16[512,2048]{1,0:T(8,128)(2,1)}, bf16[512,512]{1,0:T(8,128)(2,1)}, bf16[512,512]{1,0:T(8,128)(2,1)}) custom-call(bf16[512,1024]{1,0:T(8,128)(2,1)} %gather_project.1.keys_ref.values_ref, bf16[512,1024]{1,0:T(8,128)(2,1)} %gather_project.1.keys_ref.values_ref, bf16[512,2048]{1,0:T(8,128)(2,1)} %query_ref.1, bf16[512,2048]{1,0:T(8,128)(2,1)} %grad_ref.1, ...), custom_call_target="tpu_custom_call" | custom-call | tf_op jit(solution)/shard_map/attend/pallas_call | solution.py:304
  57.2 42.2 %gradient_reduce.1 = f32[128,128]{1,0:T(8,128)} custom-call(bf16[512,512]{1,0:T(8,128)(2,1)} %get-tuple-element.6.key_ref, bf16[512,512]{1,0:T(8,128)(2,1)} %get-tuple-element.7.value_ref, bf16[512,4096]{1,0:T(8,128)(2,1)} %hidden_hbm.3), custom_call_target="tpu_custom_call" | custom-call | tf_op jit(solution)/shard_map/gradient_reduce/pallas_call | solution.py:486
  99.4 1.5 %broadcast_multiply_fusion = f32[128,128]{1,0:T(8,128)} fusion(f32[128,128]{1,0:T(8,128)} %gradient_reduce.1, f32[]{:T(128)} %bitcast), kind=kLoop, calls=%fused_computation | loop fusion | flops 16384 | bytes 131076 | tf_op jit(solution)/shard_map/mul | solution.py:520

commit v3 on v2

--- a/solution.py
+++ b/solution.py
@@ -16,7 +16,10 @@
 NZ = 8
 STEPS = 8
 GATHER = (0, 2, 4, 6, 7)
-REDUCE = (0, 1, 3, 6, 9)
+REDUCE = (0, 1, 3, 5, 7)
+PART = 56
+CHAIN = 2
+REST = 128 - 2 * PART
 MESH = pl.DeviceIdType.MESH
 NT = (((1,), (1,)), ((), ()))
 TN = (((0,), (0,)), ((), ()))
@@ -74,21 +77,21 @@
     return barrier, len(peers)
 
 
-def pipeline(stages, starts, order):
+def pipeline(*stages):
     def body(t, carry):
-        for i in order:
-            @pl.when((t >= starts[i]) & (t < STEPS + starts[i]))
+        for stage, start, first, count in stages:
+            @pl.when((t >= start) & (t < start + count))
             def _():
-                stages[i](t - starts[i])
+                stage(t - start + first)
 
         return carry
 
-    lax.fori_loop(0, STEPS + starts[-1], body, 0)
+    lax.fori_loop(0, max(start + count for _, start, _, count in stages), body, 0)
 
 
 def project_kernel(
     start_ref, mid_ref, end_ref, time_ref, hidden_hbm, out_ref,
-    hidden, buf, acc, zs, zr, as_, ar, bs, br, ds_, dr, hsem,
+    hidden, buf, flat, acc, zs, zr, as_, ar, bs, br, ds_, dr, fs, fr, gs, gr, cs, cr, hsem,
 ):
     x, y, z, c = coordinates()
     barrier, count = greet(x, y, z, c, (1, NZ - 1))
@@ -100,8 +103,9 @@
         + 2.0 * t * (1.0 - t) * mid_ref[...].astype(F32)
         + t**2 * end_ref[...].astype(F32)
     ).astype(BF)
-    buf[0, z, c, x, y] = blended[:64]
-    buf[1, z, c, y, x] = blended[64:]
+    buf[0, z, c, x, y] = blended[:PART]
+    buf[1, z, c, y, x] = blended[PART : 2 * PART]
+    flat[z, c, x, y] = blended[2 * PART :]
     acc[...] = jnp.zeros_like(acc)
     rings = [Ring(k, x, y, z, c) for k in range(2)]
     pl.semaphore_wait(barrier, count)
@@ -139,10 +143,56 @@
         block = buf.at[k, zblock(s), c]
         return remote(block, block, ds_.at[k, s], dr.at[k, s], device(x, y, z, 1 - c))
 
+    def flat1():
+        block = flat.at[z, c, x, y]
+        return [
+            remote(block, block, fs.at[i], fr.at[i], rings[0].along1(shift)) for i, shift in enumerate((1, -1, 2))
+        ]
+
+    def flat2():
+        block = flat.at[z, c, x]
+        return [
+            remote(block, block, fs.at[3 + i], fr.at[3 + i], rings[0].along2(shift))
+            for i, shift in enumerate((1, -1, 2))
+        ]
+
+    def flatz(s):
+        sign = 2 * (s % 2) - 1
+        block = flat.at[(z + offset(s) - sign + NZ) % NZ, c]
+        return remote(block, block, gs.at[s], gr.at[s], device(x, y, (z - sign + NZ) % NZ, c))
+
+    def flatcross(s):
+        block = flat.at[zblock(s), c]
+        return remote(block, block, cs.at[s], cr.at[s], device(x, y, z, 1 - c))
+
     for s in range(1, 3):
         for k in range(2):
             zcopy(k, s).start()
+    for copy in flat1():
+        copy.start()
     load.wait()
+
+    def plane1(s):
+        for copy in flat1():
+            copy.wait_recv()
+        for copy in flat2():
+            copy.start()
+
+    def plane2(s):
+        for copy in flat2():
+            copy.wait_recv()
+        flatz(1).start()
+        flatz(2).start()
+        flatcross(0).start()
+
+    def chain(s):
+        flatz(s).wait_recv()
+
+        @pl.when(s < STEPS - 2)
+        def _():
+            flatz(s + 2).start()
+
+        flatcross(s).start()
 
     def stage0(s):
         @pl.when(s > 0)
@@ -182,23 +232,30 @@
     def stage4(s):
         for k in range(2):
             cross(k, s).wait_recv()
+        flatcross(s).wait_recv()
         zb = zblock(s)
         lhs = hidden[:, pl.ds(pl.multiple_of(zb * 512, 512), 512)]
         for n in range(4):
             groups = []
             for y_hi in range(2):
                 for core in range(2):
-                    for k in range(2):
-                        parts = []
-                        for y_lo in range(2):
-                            yy = y_hi * 2 + y_lo
-                            place = (n, yy) if k == 0 else (yy, n)
-                            parts.append(buf[k, zb, core, place[0], place[1]])
-                        groups.append(jnp.concatenate(parts, axis=1))
+                    pair = (y_hi * 2, y_hi * 2 + 1)
+                    groups.append(jnp.concatenate([buf[0, zb, core, n, yy] for yy in pair], axis=1))
+                    groups.append(jnp.concatenate([buf[1, zb, core, yy, n] for yy in pair], axis=1))
+                    groups.append(jnp.concatenate([flat[zb, core, n, yy] for yy in pair], axis=1))
             rhs = jnp.concatenate(groups, axis=0)
             acc[:, n * 256 : (n + 1) * 256] += jnp.dot(lhs, rhs, preferred_element_type=F32)
 
-    pipeline((stage0, stage1, stage2, stage3, stage4), GATHER, range(5))
+    pipeline(
+        (stage0, GATHER[0], 0, STEPS),
+        (stage1, GATHER[1], 0, STEPS),
+        (stage2, GATHER[2], 0, STEPS),
+        (stage3, GATHER[3], 0, STEPS),
+        (plane1, 1, 0, 1),
+        (plane2, 3, 0, 1),
+        (chain, 6, 1, STEPS - 1),
+        (stage4, GATHER[4], 0, STEPS),
+    )
     out_ref[...] = acc[...].astype(BF)
 
     def drain(s, carry):
@@ -209,9 +266,17 @@
 
             for copy in first(k, s) + near(k, s) + far(k, s) + [cross(k, s)]:
                 copy.wait_send()
+
+        @pl.when(s > 0)
+        def _():
+            flatz(s).wait_send()
+
+        flatcross(s).wait_send()
         return carry
 
     lax.fori_loop(0, STEPS, drain, 0)
+    for copy in flat1() + flat2():
+        copy.wait_send()
 
 
 def project(start, mid, end, time, hidden):
@@ -225,12 +290,16 @@
         out_specs=vmem,
         scratch_shapes=[
             pltpu.VMEM((SEQ, 4096), BF),
-            pltpu.VMEM((2, NZ, 2, 4, 4, 64, 128), BF),
+            pltpu.VMEM((2, NZ, 2, 4, 4, PART, 128), BF),
+            pltpu.VMEM((NZ, 2, 4, 4, REST, 128), BF),
             pltpu.VMEM((SEQ, 1024), F32),
             dma((2, STEPS)), dma((2, STEPS)),
             dma((2, STEPS, 3)), dma((2, STEPS, 3)),
             dma((2, STEPS, 4)), dma((2, STEPS, 4)),
             dma((2, STEPS)), dma((2, STEPS)),
+            dma((6,)), dma((6,)),
+            dma((STEPS,)), dma((STEPS,)),
+            dma((STEPS,)), dma((STEPS,)),
             dma(()),
         ],
         compiler_params=pltpu.CompilerParams(collective_id=0, has_side_effects=True, vmem_limit_bytes=60 * 2**20),
@@ -328,18 +397,24 @@
 
 
 def reduce_kernel(
-    key_ref, value_ref, hidden_hbm, out_ref,
+    key_ref, value_ref, time_ref, hidden_hbm, out_ref,
     hidden, dsend, drecv, own, total, farr, nearr, mid, firstr, zsend, zrecv, last,
-    ds_, dr, bs, br, as_, ar, zs, zr, hsem,
+    fsend, frecv, fown, flat, flatr, slabr, line, liner,
+    ds_, dr, bs, br, as_, ar, zs, zr, cs, cr, gs, gr, fs, fr, hsem,
 ):
     x, y, z, c = coordinates()
     barrier, count = greet(x, y, z, c, range(1, NZ))
-    load = pltpu.make_async_copy(hidden_hbm, hidden, hsem)
-    load.start()
     rings = [Ring(k, x, y, z, c) for k in range(2)]
 
     def target(s):
         return (z + offset(7 - s) + NZ) % NZ
+
+    def load(s):
+        columns = pl.ds(pl.multiple_of(target(s) * 512, 512), 512)
+        return pltpu.make_async_copy(hidden_hbm.at[:, columns], hidden.at[:, columns], hsem.at[s])
+
+    for s in range(STEPS):
+        load(s).start()
 
     def cross(k, s):
         return remote(dsend.at[s, k], drecv.at[s, k], ds_.at[k, s], dr.at[k, s], device(x, y, z, 1 - c))
@@ -374,6 +449,28 @@
 
     def zcopy(k, s):
         return remote(zsend.at[s, k], zrecv.at[s, k], zs.at[k, s], zr.at[k, s], device(x, y, target(s), c))
+
+    def flatcross(s):
+        return remote(fsend.at[s], frecv.at[s], cs.at[s], cr.at[s], device(x, y, z, 1 - c))
+
+    def flatz(s):
+        return remote(
+            flat.at[s], flatr.at[s], gs.at[s], gr.at[s], device(x, y, (z + 1 - 2 * (s % 2) + NZ) % NZ, c)
+        )
+
+    def flat2():
+        return [
+            remote(
+                flat.at[STEPS - 1, (x + shift + 4) % 4], slabr.at[i], fs.at[i], fr.at[i], rings[0].along2(shift)
+            )
+            for i, shift in enumerate((1, -1, 2))
+        ]
+
+    def flat1():
+        return [
+            remote(line.at[(y + shift + 4) % 4], liner.at[i], fs.at[3 + i], fr.at[3 + i], rings[0].along1(shift))
+            for i, shift in enumerate((1, -1, 2))
+        ]
 
     def product(s, core, store):
         base = target(s) * 512 + core * 128
@@ -387,25 +484,35 @@
                 for y_hi in range(2):
                     yy = y_hi * 2 + row % 2
                     lanes = slice(y_hi * 128, (y_hi + 1) * 128)
-                    store(0, xx, yy, grads[row * 128 : row * 128 + 64, lanes])
-                    store(1, yy, xx, grads[row * 128 + 64 : row * 128 + 128, lanes])
+                    block = grads[row * 128 : row * 128 + 128, lanes]
+                    store(0, xx, yy, block[:PART])
+                    store(1, yy, xx, block[PART : 2 * PART])
+                    store(2, xx, yy, block[2 * PART :])
 
     def give(s):
         def away(k, i, j, block):
-            dsend[s, k, i, j] = block.astype(BF)
+            if k < 2:
+                dsend[s, k, i, j] = block.astype(BF)
+            else:
+                fsend[s, i, j] = block.astype(BF)
 
         product(s, 1 - c, away)
 
     def stage0(s):
         def keep(k, i, j, block):
-            own[s % 4, k, i, j] = block
+            if k < 2:
+                own[s % 4, k, i, j] = block
+            else:
+                fown[s % 4, i, j] = block
 
         @pl.when(s > 0)
         def _():
+            load(s).wait()
             give(s)
 
         for k in range(2):
             cross(k, s).start()
+        flatcross(s).start()
         product(s, c, keep)
 
     def stage1(s):
@@ -454,10 +561,59 @@
             for k in range(2):
                 zcopy(k, s).start()
 
-    load.wait()
+    def chain(s):
+        flatcross(s).wait_recv()
+
+        def gathered(extra):
+            for place in range(4):
+                value = fown[s % 4, place] + frecv[s, place].astype(F32)
+                for step in extra:
+                    value = value + flatr[step, place].astype(F32)
+                flat[s, place] = value.astype(BF)
+
+        @pl.when(s < 2)
+        def _():
+            gathered(())
+
+        @pl.when((s >= 2) & (s < STEPS - 1))
+        def _():
+            flatz(s - 2).wait_recv()
+            gathered((s - 2,))
+
+        @pl.when(s < STEPS - 1)
+        def _():
+            flatz(s).start()
+
+        @pl.when(s == STEPS - 1)
+        def _():
+            flatz(STEPS - 3).wait_recv()
+            flatz(STEPS - 2).wait_recv()
+            gathered((STEPS - 3, STEPS - 2))
+            for copy in flat2():
+                copy.start()
+
+    def plane2(s):
+        for copy in flat2():
+            copy.wait_recv()
+        value = flat[STEPS - 1, x].astype(F32)
+        for i in range(3):
+            value = value + slabr[i].astype(F32)
+        line[...] = value.astype(BF)
+        for copy in flat1():
+            copy.start()
+
+    load(0).wait()
     give(0)
     pl.semaphore_wait(barrier, count)
-    pipeline((stage0, stage1, stage2, stage3, stage4), REDUCE, (2, 1, 3, 4, 0))
+    pipeline(
+        (stage2, REDUCE[2], 0, STEPS),
+        (stage1, REDUCE[1], 0, STEPS),
+        (stage3, REDUCE[3], 0, STEPS),
+        (stage4, REDUCE[4], 0, STEPS),
+        (chain, CHAIN, 0, STEPS),
+        (plane2, CHAIN + STEPS + 1, 0, 1),
+        (stage0, REDUCE[0], 0, STEPS),
+    )
     sums = []
     for k in range(2):
         value = last[k]
@@ -465,7 +621,14 @@
             zcopy(k, s).wait_recv()
             value = value + zrecv[s, k].astype(F32)
         sums.append(value)
-    out_ref[...] = jnp.concatenate(sums, axis=0).T
+    for copy in flat1():
+        copy.wait_recv()
+    value = line[y].astype(F32)
+    for i in range(3):
+        value = value + liner[i].astype(F32)
+    sums.append(value)
+    t = time_ref[0]
+    out_ref[...] = jnp.concatenate(sums, axis=0).T * (2.0 * t * (1.0 - t))
 
     def drain(s, carry):
         for k in range(2):
@@ -475,49 +638,66 @@
 
             for copy in first(k, s) + near(k, s) + far(k, s) + [cross(k, s)]:
                 copy.wait_send()
+
+        @pl.when(s < STEPS - 1)
+        def _():
+            flatz(s).wait_send()
+
+        flatcross(s).wait_send()
         return carry
 
     lax.fori_loop(0, STEPS, drain, 0)
-
-
-def reduce(key_grad, value_grad, hidden):
+    for copy in flat1() + flat2():
+        copy.wait_send()
+
+
+def reduce(key_grad, value_grad, time, hidden):
     vmem = pl.BlockSpec(memory_space=pltpu.VMEM)
     dma = pltpu.SemaphoreType.DMA
     return pl.pallas_call(
         reduce_kernel,
         name="gradient_reduce",
         out_shape=jax.ShapeDtypeStruct((128, 128), F32),
-        in_specs=[vmem, vmem, pl.BlockSpec(memory_space=pl.ANY)],
+        in_specs=[vmem, vmem, pl.BlockSpec(memory_space=pltpu.SMEM), pl.BlockSpec(memory_space=pl.ANY)],
         out_specs=vmem,
         scratch_shapes=[
             pltpu.VMEM((SEQ, 4096), BF),
-            pltpu.VMEM((STEPS, 2, 4, 4, 64, 128), BF),
-            pltpu.VMEM((STEPS, 2, 4, 4, 64, 128), BF),
-            pltpu.VMEM((4, 2, 4, 4, 64, 128), F32),
-            pltpu.VMEM((STEPS, 2, 4, 4, 64, 128), BF),
-            pltpu.VMEM((STEPS, 2, 4, 64, 128), BF),
-            pltpu.VMEM((STEPS, 2, 2, 4, 64, 128), BF),
-            pltpu.VMEM((STEPS, 2, 4, 64, 128), BF),
-            pltpu.VMEM((STEPS, 2, 3, 64, 128), BF),
-            pltpu.VMEM((STEPS, 2, 64, 128), BF),
-            pltpu.VMEM((STEPS, 2, 64, 128), BF),
-            pltpu.VMEM((2, 64, 128), F32),
+            pltpu.VMEM((STEPS, 2, 4, 4, PART, 128), BF),
+            pltpu.VMEM((STEPS, 2, 4, 4, PART, 128), BF),
+            pltpu.VMEM((4, 2, 4, 4, PART, 128), F32),
+            pltpu.VMEM((STEPS, 2, 4, 4, PART, 128), BF),
+            pltpu.VMEM((STEPS, 2, 4, PART, 128), BF),
+            pltpu.VMEM((STEPS, 2, 2, 4, PART, 128), BF),
+            pltpu.VMEM((STEPS, 2, 4, PART, 128), BF),
+            pltpu.VMEM((STEPS, 2, 3, PART, 128), BF),
+            pltpu.VMEM((STEPS, 2, PART, 128), BF),
+            pltpu.VMEM((STEPS, 2, PART, 128), BF),
+            pltpu.VMEM((2, PART, 128), F32),
+            pltpu.VMEM((STEPS, 4, 4, REST, 128), BF),
+            pltpu.VMEM((STEPS, 4, 4, REST, 128), BF),
+            pltpu.VMEM((4, 4, 4, REST, 128), F32),
+            pltpu.VMEM((STEPS, 4, 4, REST, 128), BF),
+            pltpu.VMEM((STEPS, 4, 4, REST, 128), BF),
+            pltpu.VMEM((3, 4, REST, 128), BF),
+            pltpu.VMEM((4, REST, 128), BF),
+            pltpu.VMEM((3, REST, 128), BF),
             dma((2, STEPS)), dma((2, STEPS)),
             dma((2, STEPS, 4)), dma((2, STEPS, 4)),
             dma((2, STEPS, 3)), dma((2, STEPS, 3)),
             dma((2, STEPS)), dma((2, STEPS)),
-            dma(()),
+            dma((STEPS,)), dma((STEPS,)),
+            dma((STEPS,)), dma((STEPS,)),
+            dma((6,)), dma((6,)),
+            dma((STEPS,)),
         ],
         compiler_params=pltpu.CompilerParams(collective_id=1, has_side_effects=True, vmem_limit_bytes=60 * 2**20),
-    )(key_grad, value_grad, hidden)
+    )(key_grad, value_grad, time, hidden)
 
 
 def local(hidden, queries, cotangent, point_start, point_mid, point_end, curve_time):
     kv = project(point_start, point_mid, point_end, curve_time, hidden)
     context, key_grad, value_grad = attend(kv, queries, cotangent)
-    gradient = reduce(key_grad, value_grad, hidden)
-    t_value = curve_time[0]
-    return (context, gradient * (2.0 * t_value * (1.0 - t_value)))
+    return context, reduce(key_grad, value_grad, curve_time, hidden)
 
 
 def solution(mesh):

time: 101 us -> 98.2 us (0.972)
  Pallas kernels: 98.1 us -> 95.2 us
  other arithmetic: 1.48 us -> 0 us
  local copies, waits for them, and re-layouts: 0 us -> 1.47 us
    pallas_call x1, Pallas kernels: 42.2 us -> 40.7 us  [reduce(): pl.pallas_call(reduce_kernel, name='gradient_reduce', out_shape=jax.Shape...]
    mul x1 -> x0, other arithmetic: 1.48 us -> none  [local(): return (context, gradient * (2.0 * t_value * (1.0 - t_value)))]
    pallas_call x1, Pallas kernels: 42.1 us -> 40.6 us  [project(): pl.pallas_call(project_kernel, name='gather_project', out_shape=jax.Shape...]
    unnamed x0 -> x1, local copies, waits for them, and re-layouts: none -> 1.47 us
where the time goes in v3:
time: 98.2 us; the launch traced here: 97.9 us
  Pallas kernels  95.2 us (97%)
  local copies, waits for them, and re-layouts  1.47 us (1%)
  between operations  1.29 us (1%)
    pallas_call x1, Pallas kernels, reduce(): pl.pallas_call(reduce_kernel, name='gradient_reduce', out_shape=jax.Shape...  40.7 us
    pallas_call x1, Pallas kernels, project(): pl.pallas_call(project_kernel, name='gather_project', out_shape=jax.Shape...  40.6 us
    pallas_call x1, Pallas kernels, attend(): pl.pallas_call(attend_kernel, name='attend', grid=(KVH,), out_shape=(jax....  13.8 us

profile of v3, /device:TPU:2, one launch (start us, length us, event | category | flops | bytes accessed | tf_op | source)
XLA Modules:
  0.0 97.9 jit_solution(2972017181309376284)
XLA Ops:
  1.3 40.6 %gather_project.1.keys_ref.values_ref = bf16[512,1024]{1,0:T(8,128)(2,1)} custom-call(bf16[128,128]{1,0:T(8,128)(2,1)} %start_ref.1, bf16[128,128]{1,0:T(8,128)(2,1)} %mid_ref.1, bf16[128,128]{1,0:T(8,128)(2,1)} %end_ref.1, f32[1]{0:T(128)S(6)} %copy.14.time_ref, bf16[512,4096]{1,0:T(8,128)(2,1)} %hidden_hbm.3), custom_call_target="tpu_custom_call" | custom-call | tf_op jit(solution)/shard_map/gather_project/pallas_call | solution.py:285
  41.9 13.8 %attend.1 = (bf16[512,2048]{1,0:T(8,128)(2,1)}, bf16[512,512]{1,0:T(8,128)(2,1)}, bf16[512,512]{1,0:T(8,128)(2,1)}) custom-call(bf16[512,1024]{1,0:T(8,128)(2,1)} %gather_project.1.keys_ref.values_ref, bf16[512,1024]{1,0:T(8,128)(2,1)} %gather_project.1.keys_ref.values_ref, bf16[512,2048]{1,0:T(8,128)(2,1)} %query_ref.1, bf16[512,2048]{1,0:T(8,128)(2,1)} %grad_ref.1, ...), custom_call_target="tpu_custom_call" | custom-call | tf_op jit(solution)/shard_map/attend/pallas_call | solution.py:373
  55.7 40.7 %gradient_reduce.1 = f32[128,128]{1,0:T(8,128)} custom-call(bf16[512,512]{1,0:T(8,128)(2,1)} %get-tuple-element.6.key_ref, bf16[512,512]{1,0:T(8,128)(2,1)} %get-tuple-element.7.value_ref, f32[1]{0:T(128)S(6)} %copy.14.time_ref, bf16[512,4096]{1,0:T(8,128)(2,1)} %hidden_hbm.3), custom_call_target="tpu_custom_call" | custom-call | tf_op jit(solution)/shard_map/gradient_reduce/pallas_call | solution.py:657
  96.5 1.5 %copy.15 = f32[128,128]{1,0:T(8,128)} copy(f32[128,128]{1,0:T(8,128)} %gradient_reduce.1) | data formatting | bytes 131072

commit v4 on v3

--- a/solution.py
+++ b/solution.py
@@ -139,9 +139,9 @@
             copies.append(remote(block, block, bs.at[k, s, 2 + i], br.at[k, s, 2 + i], rings[k].along2(shift)))
         return copies
 
-    def cross(k, s):
-        block = buf.at[k, zblock(s), c]
-        return remote(block, block, ds_.at[k, s], dr.at[k, s], device(x, y, z, 1 - c))
+    def cross(k, s, shift):
+        block = buf.at[k, zblock(s), c, (rings[k].p2 + shift + 4) % 4]
+        return remote(block, block, ds_.at[k, s, shift + 1], dr.at[k, s, shift + 1], device(x, y, z, 1 - c))
 
     def flat1():
         block = flat.at[z, c, x, y]
@@ -215,6 +215,7 @@
                 copy.wait_recv()
             for copy in near(k, s):
                 copy.start()
+            cross(k, s, 0).start()
 
     def stage2(s):
         for k in range(2):
@@ -222,16 +223,19 @@
                 copy.wait_recv()
             for copy in far(k, s):
                 copy.start()
+            cross(k, s, -1).start()
+            cross(k, s, 1).start()
 
     def stage3(s):
         for k in range(2):
             for copy in far(k, s):
                 copy.wait_recv()
-            cross(k, s).start()
+            cross(k, s, 2).start()
 
     def stage4(s):
         for k in range(2):
-            cross(k, s).wait_recv()
+            for shift in range(-1, 3):
+                cross(k, s, shift).wait_recv()
         flatcross(s).wait_recv()
         zb = zblock(s)
         lhs = hidden[:, pl.ds(pl.multiple_of(zb * 512, 512), 512)]
@@ -264,8 +268,10 @@
             def _():
                 zcopy(k, s).wait_send()
 
-            for copy in first(k, s) + near(k, s) + far(k, s) + [cross(k, s)]:
+            for copy in first(k, s) + near(k, s) + far(k, s):
                 copy.wait_send()
+            for shift in range(-1, 3):
+                cross(k, s, shift).wait_send()
 
         @pl.when(s > 0)
         def _():
@@ -296,7 +302,7 @@
             dma((2, STEPS)), dma((2, STEPS)),
             dma((2, STEPS, 3)), dma((2, STEPS, 3)),
             dma((2, STEPS, 4)), dma((2, STEPS, 4)),
-            dma((2, STEPS)), dma((2, STEPS)),
+            dma((2, STEPS, 4)), dma((2, STEPS, 4)),
             dma((6,)), dma((6,)),
             dma((STEPS,)), dma((STEPS,)),
             dma((STEPS,)), dma((STEPS,)),

time: 98.2 us -> 98.8 us (level)
  no operation moved by 1% of the time
where the time goes in v4:
time: 98.8 us; the launch traced here: 98.3 us
  Pallas kernels  95.6 us (97%)
  local copies, waits for them, and re-layouts  1.47 us (1%)
  between operations  1.29 us (1%)
    pallas_call x1, Pallas kernels, project(): pl.pallas_call(project_kernel, name='gather_project', out_shape=jax.Shape...  41.6 us
    pallas_call x1, Pallas kernels, reduce(): pl.pallas_call(reduce_kernel, name='gradient_reduce', out_shape=jax.Shape...  40.2 us
    pallas_call x1, Pallas kernels, attend(): pl.pallas_call(attend_kernel, name='attend', grid=(KVH,), out_shape=(jax....  13.8 us

profile of v4, /device:TPU:2, one launch (start us, length us, event | category | flops | bytes accessed | tf_op | source)
XLA Modules:
  0.0 98.3 jit_solution(13552289466262461555)
XLA Ops:
  1.3 41.6 %gather_project.1.keys_ref.values_ref = bf16[512,1024]{1,0:T(8,128)(2,1)} custom-call(bf16[128,128]{1,0:T(8,128)(2,1)} %start_ref.1, bf16[128,128]{1,0:T(8,128)(2,1)} %mid_ref.1, bf16[128,128]{1,0:T(8,128)(2,1)} %end_ref.1, f32[1]{0:T(128)S(6)} %copy.14.time_ref, bf16[512,4096]{1,0:T(8,128)(2,1)} %hidden_hbm.3), custom_call_target="tpu_custom_call" | custom-call | tf_op jit(solution)/shard_map/gather_project/pallas_call | solution.py:291
  42.9 13.8 %attend.1 = (bf16[512,2048]{1,0:T(8,128)(2,1)}, bf16[512,512]{1,0:T(8,128)(2,1)}, bf16[512,512]{1,0:T(8,128)(2,1)}) custom-call(bf16[512,1024]{1,0:T(8,128)(2,1)} %gather_project.1.keys_ref.values_ref, bf16[512,1024]{1,0:T(8,128)(2,1)} %gather_project.1.keys_ref.values_ref, bf16[512,2048]{1,0:T(8,128)(2,1)} %query_ref.1, bf16[512,2048]{1,0:T(8,128)(2,1)} %grad_ref.1, ...), custom_call_target="tpu_custom_call" | custom-call | tf_op jit(solution)/shard_map/attend/pallas_call | solution.py:379
  56.7 40.2 %gradient_reduce.1 = f32[128,128]{1,0:T(8,128)} custom-call(bf16[512,512]{1,0:T(8,128)(2,1)} %get-tuple-element.6.key_ref, bf16[512,512]{1,0:T(8,128)(2,1)} %get-tuple-element.7.value_ref, f32[1]{0:T(128)S(6)} %copy.14.time_ref, bf16[512,4096]{1,0:T(8,128)(2,1)} %hidden_hbm.3), custom_call_target="tpu_custom_call" | custom-call | tf_op jit(solution)/shard_map/gradient_reduce/pallas_call | solution.py:663
  96.9 1.5 %copy.15 = f32[128,128]{1,0:T(8,128)} copy(f32[128,128]{1,0:T(8,128)} %gradient_reduce.1) | data formatting | bytes 131072

commit v5 on v3

--- a/solution.py
+++ b/solution.py
@@ -330,18 +330,19 @@
         query = jnp.concatenate([query_ref[rows, h * HD : (h + 1) * HD] for h in range(4)], axis=0)
         grad = jnp.concatenate([grad_ref[rows, h * HD : (h + 1) * HD] for h in range(4)], axis=0)
         scores = lax.dot_general(query, k_t, NT, preferred_element_type=F32)
-        dprobs = lax.dot_general(grad, v_t, NT, preferred_element_type=F32)
         diagonal = jnp.where(causal, scores[:, length - ROWS :], -1e30)
         scores = diagonal if tile == 0 else jnp.concatenate([scores[:, : length - ROWS], diagonal], axis=1)
         top = jnp.max(scores, axis=-1, keepdims=True)
         weights = jnp.exp2((scores - top) * FOLD)
-        probs = weights * (1.0 / jnp.sum(weights, axis=-1, keepdims=True))
-        low = probs.astype(BF)
-        context = jnp.dot(low, v_t, preferred_element_type=F32)
+        low = weights.astype(BF)
+        scale = 1.0 / jnp.sum(weights, axis=-1, keepdims=True)
+        context = jnp.dot(low, v_t, preferred_element_type=F32) * scale
         for h in range(4):
             context_ref[rows, h * HD : (h + 1) * HD] = context[h * ROWS : (h + 1) * ROWS].astype(BF)
+        grad = (grad.astype(F32) * scale).astype(BF)
+        dprobs = lax.dot_general(grad, v_t, NT, preferred_element_type=F32)
         inner = jnp.sum(context * grad.astype(F32), axis=-1, keepdims=True)
-        dscores = (probs * (dprobs - inner)).astype(BF)
+        dscores = (weights * (dprobs - inner)).astype(BF)
         value_acc[:, :length] += lax.dot_general(grad, low, TN, preferred_element_type=F32)
         key_acc[:, :length] += lax.dot_general(query, dscores, TN, preferred_element_type=F32)
     value_grad_ref[...] = value_acc[...].astype(BF)

time: 98.2 us -> 97.4 us (level)
  no operation moved by 1% of the time
where the time goes in v5:
time: 97.4 us; the launch traced here: 97.1 us
  Pallas kernels  94.4 us (97%)
  local copies, waits for them, and re-layouts  1.47 us (2%)
  between operations  1.29 us (1%)
    pallas_call x1, Pallas kernels, reduce(): pl.pallas_call(reduce_kernel, name='gradient_reduce', out_shape=jax.Shape...  40.7 us
    pallas_call x1, Pallas kernels, project(): pl.pallas_call(project_kernel, name='gather_project', out_shape=jax.Shape...  40.6 us
    pallas_call x1, Pallas kernels, attend(): pl.pallas_call(attend_kernel, name='attend', grid=(KVH,), out_shape=(jax....  13.1 us

profile of v5, /device:TPU:2, one launch (start us, length us, event | category | flops | bytes accessed | tf_op | source)
XLA Modules:
  0.0 97.1 jit_solution(14930635884394433216)
XLA Ops:
  1.3 40.6 %gather_project.1.keys_ref.values_ref = bf16[512,1024]{1,0:T(8,128)(2,1)} custom-call(bf16[128,128]{1,0:T(8,128)(2,1)} %start_ref.1, bf16[128,128]{1,0:T(8,128)(2,1)} %mid_ref.1, bf16[128,128]{1,0:T(8,128)(2,1)} %end_ref.1, f32[1]{0:T(128)S(6)} %copy.14.time_ref, bf16[512,4096]{1,0:T(8,128)(2,1)} %hidden_hbm.3), custom_call_target="tpu_custom_call" | custom-call | tf_op jit(solution)/shard_map/gather_project/pallas_call | solution.py:285
  41.9 13.1 %attend.1 = (bf16[512,2048]{1,0:T(8,128)(2,1)}, bf16[512,512]{1,0:T(8,128)(2,1)}, bf16[512,512]{1,0:T(8,128)(2,1)}) custom-call(bf16[512,1024]{1,0:T(8,128)(2,1)} %gather_project.1.keys_ref.values_ref, bf16[512,1024]{1,0:T(8,128)(2,1)} %gather_project.1.keys_ref.values_ref, bf16[512,2048]{1,0:T(8,128)(2,1)} %query_ref.1, bf16[512,2048]{1,0:T(8,128)(2,1)} %grad_ref.1, ...), custom_call_target="tpu_custom_call" | custom-call | tf_op jit(solution)/shard_map/attend/pallas_call | solution.py:374
  54.9 40.7 %gradient_reduce.1 = f32[128,128]{1,0:T(8,128)} custom-call(bf16[512,512]{1,0:T(8,128)(2,1)} %get-tuple-element.6.key_ref, bf16[512,512]{1,0:T(8,128)(2,1)} %get-tuple-element.7.value_ref, f32[1]{0:T(128)S(6)} %copy.14.time_ref, bf16[512,4096]{1,0:T(8,128)(2,1)} %hidden_hbm.3), custom_call_target="tpu_custom_call" | custom-call | tf_op jit(solution)/shard_map/gradient_reduce/pallas_call | solution.py:658
  95.7 1.5 %copy.15 = f32[128,128]{1,0:T(8,128)} copy(f32[128,128]{1,0:T(8,128)} %gradient_reduce.1) | data formatting | bytes 131072
